TPU v7x, 32 devices: a whole 2x2x4 slice. The times are simulated.
32 devices in a mesh: seq: 8 (over y, x, core), head: 4 (over z).
Axes of the slice: x: 2, y: 2, z: 4, core: 2. Of those that a mesh axis runs over, the one named last changes fastest.
Arguments:
- queries: bfloat16 [2048, 2048], P('seq', 'head'), may hold values from -6 to 6
- key_vectors: bfloat16 [2048, 2048], P('seq', 'head'), may hold values from -6 to 6
- value_vectors: bfloat16 [2048, 4096], P('seq', 'head'), may hold values from -8 to 8
- out_weight: bfloat16 [4096, 4096], P('head'), may hold values from -0.125 to 0.125
Outputs:
- mixed: bfloat16 [2048, 4096], P('seq', 'head')
All inputs are finite; a program needn't handle non-finite values.
Results may differ from a plain program's by a relative error of at most 0.008.
Values may be sent and summed in bfloat16 or wider, within the bound.
No kernel may reach another device: no remote copies, remote signals or barrier semaphores. Data moves between devices by JAX's collectives and lax.ppermute only.
A program may use at most 256 MiB of HBM per device.

v0:
```python
import functools

import jax
import jax.numpy as jnp
from jax import lax
from jax.experimental import pallas as pl
from jax.experimental.pallas import tpu as pltpu
from jax.sharding import PartitionSpec as P


KD = 64
VD = 128


def swap(value, axis, bits):
    count = lax.axis_size(axis)
    return lax.ppermute(value, axis, [(i, i ^ bits) for i in range(count)])


def in_vmem(*values):
    return [pltpu.with_memory_space_constraint(value, pltpu.VMEM) for value in values]


def in_hbm(*values):
    return [pltpu.with_memory_space_constraint(value, pltpu.HBM) for value in values]


def room(mebibytes):
    return pltpu.CompilerParams(vmem_limit_bytes=mebibytes << 20)


def seat():
    here = lax.axis_index("seq")
    return here >> 1, here & 1


def pack_kernel(q_ref, k_ref, v_ref, *refs):
    outs, arrived = refs[:-1], refs[-1]
    wide_k = outs[0].shape[1] // 4
    here, _ = seat()
    copies = []
    for turn in (*range(1, len(outs)), 0):
        at = 0
        for source, wide in ((q_ref, wide_k), (k_ref, wide_k), (v_ref, 2 * wide_k)):
            columns = pl.ds(pl.multiple_of((here ^ turn) * wide, wide), wide)
            copies.append(
                pltpu.make_async_copy(
                    source.at[:, columns], outs[turn].at[:, at : at + wide], arrived.at[len(copies)]
                )
            )
            at += wide
    for copy in copies:
        copy.start()
    for copy in copies:
        copy.wait()


def pack(queries, keys, values, chips):
    length, width = queries.shape
    each = pltpu.VMEM((length, 4 * width // chips), queries.dtype)
    return pl.pallas_call(
        pack_kernel,
        out_shape=(each,) * chips,
        in_specs=[pl.BlockSpec(memory_space=pltpu.HBM)] * 3,
        scratch_shapes=[pltpu.SemaphoreType.DMA((3 * chips,))],
        compiler_params=room(8),
        name="pack",
    )(*in_hbm(queries, keys, values))


def stage_kernel(w_ref, out, arrived):
    copy = pltpu.make_async_copy(w_ref, out, arrived.at[0])
    copy.start()
    copy.wait()


def stage(weight):
    return pl.pallas_call(
        stage_kernel,
        out_shape=pltpu.VMEM(weight.shape, weight.dtype),
        in_specs=[pl.BlockSpec(memory_space=pltpu.HBM)],
        scratch_shapes=[pltpu.SemaphoreType.DMA((1,))],
        compiler_params=room(4),
        name="stage",
    )(*in_hbm(weight))


def attend_rows(q_all, k_all, v_all, o_all, rows_from, core, chips, heads):
    length, wide_k = k_all.shape[0] // (2 * chips), heads * KD
    count = o_all.shape[0] // chips
    row = lax.broadcasted_iota(jnp.int32, (count, 2 * length), 0) + (core * length + rows_from)
    seen = lax.broadcasted_iota(jnp.int32, (count, 2 * length), 1) <= row
    lane = lax.broadcasted_iota(jnp.int32, (count, wide_k), 1) // KD
    for index in range(chips):
        at = index * length + rows_from
        q = q_all[at : at + count, :] * jnp.bfloat16(KD ** (-0.5))
        for head in range(heads):
            own = jnp.where(lane == head, q, jnp.bfloat16(0))
            columns = slice(2 * head * VD, (2 * head + 2) * VD)
            total = None
            for block in range(index + 1):
                rows = slice(2 * block * length, 2 * (block + 1) * length)
                scores = lax.dot_general(
                    own, k_all[rows, :], (((1,), (1,)), ((), ())), preferred_element_type=jnp.float32
                )
                raised = scores + 1.0
                weights = raised * raised + 1.0
                if block == index:
                    weights = jnp.where(seen, weights, 0.0)
                part = jnp.dot(
                    weights.astype(jnp.bfloat16), v_all[rows, columns], preferred_element_type=jnp.float32
                )
                total = part if total is None else total + part
            o_all[index * count : (index + 1) * count, head * VD : (head + 1) * VD] = (
                total[:, :VD] / total[:, VD:]
            ).astype(jnp.bfloat16)


def deal(o_all, outs, chip):
    count = outs[0].shape[0]
    for turn, out in enumerate(outs):
        out[...] = o_all[pl.ds(pl.multiple_of((chip ^ turn) * count, count), count), :]


def attend_first_kernel(*refs, chips, heads):
    mine, partner = refs[:chips], refs[chips : 2 * chips]
    outs, (q_all, k_all, v_all) = refs[2 * chips : 3 * chips], refs[3 * chips : 3 * chips + 3]
    o_all = refs[-1]
    length = mine[0].shape[0]
    wide_k = heads * KD
    chip, core = seat()
    ones = jnp.ones((length, VD), jnp.bfloat16)
    for turn in range(chips):
        there = chip ^ turn
        q_all[pl.ds(pl.multiple_of(there * length, length), length), :] = mine[turn][:, :wide_k]
        for ref, side in ((mine[turn], core), (partner[turn], 1 - core)):
            rows = pl.ds(pl.multiple_of((2 * there + side) * length, length), length)
            k_all[rows, :] = ref[:, wide_k : 2 * wide_k]
            for head in range(heads):
                at = 2 * wide_k + head * VD
                v_all[rows, 2 * head * VD : (2 * head + 1) * VD] = ref[:, at : at + VD]
                v_all[rows, (2 * head + 1) * VD : (2 * head + 2) * VD] = ones
    attend_rows(q_all, k_all, v_all, o_all, 0, core, chips, heads)
    deal(o_all, outs, chip)


def attend_later_kernel(q_all, k_all, v_all, *refs, chips, heads, rows_from):
    chip, core = seat()
    attend_rows(q_all, k_all, v_all, refs[-1], rows_from, core, chips, heads)
    deal(refs[-1], refs[:-1], chip)


def attend(mine, partner, heads, cuts):
    chips, (length, _), kind = len(mine), mine[0].shape, mine[0].dtype
    whole, sizes = 2 * chips * length, [high - low for low, high in zip(cuts, cuts[1:])]
    each = [pltpu.VMEM((size, heads * VD), kind) for size in sizes]
    *first, q_all, k_all, v_all = pl.pallas_call(
        functools.partial(attend_first_kernel, chips=chips, heads=heads),
        out_shape=(
            *(each[0],) * chips,
            pltpu.VMEM((whole // 2, heads * KD), kind),
            pltpu.VMEM((whole, heads * KD), kind),
            pltpu.VMEM((whole, 2 * heads * VD), kind),
        ),
        scratch_shapes=[pltpu.VMEM((chips * sizes[0], heads * VD), kind)],
        compiler_params=room(20),
        name="attend0",
    )(*in_vmem(*mine, *partner))
    results = [first]
    for part in range(1, len(sizes)):
        results.append(
            pl.pallas_call(
                functools.partial(attend_later_kernel, chips=chips, heads=heads, rows_from=cuts[part]),
                out_shape=(each[part],) * chips,
                scratch_shapes=[pltpu.VMEM((chips * sizes[part], heads * VD), kind)],
                compiler_params=room(16),
            )(*in_vmem(q_all, k_all, v_all))
        )
    return results


def block_at(slot):
    rank = lax.axis_index("head")
    turns = [(3, 3, 0, 0), (2, 2, 1, 1), (1, 0, 3, 2), (0, 1, 2, 3)][slot]
    block = jnp.int32(turns[0])
    for other in range(1, 4):
        block = jnp.where(rank == other, jnp.int32(turns[other]), block)
    return block


def project_kernel(*refs, chips, chunks, jobs):
    pieces, w_ref, outs = refs[: chunks * chips], refs[chunks * chips], refs[chunks * chips + 1 :]
    depth, columns = pieces[0].shape[1], outs[0].shape[1]
    here, _ = seat()
    for (slot, wanted), out in zip(jobs, outs):
        at = pl.ds(pl.multiple_of(block_at(slot) * columns, columns), columns)
        low = 0
        for chunk in wanted:
            total = None
            for turn in range(chips):
                rows = pl.ds(pl.multiple_of((here ^ turn) * depth, depth), depth)
                part = jnp.dot(
                    pieces[chunk * chips + turn][...], w_ref[rows, at], preferred_element_type=jnp.float32
                )
                total = part if total is None else total + part
            out[low : low + total.shape[0], :] = total.astype(out.dtype)
            low += total.shape[0]


def project(chunks, weight, columns, jobs, kinds):
    sizes = [pieces[0].shape[0] for pieces in chunks]
    return pl.pallas_call(
        functools.partial(project_kernel, chips=len(chunks[0]), chunks=len(chunks), jobs=jobs),
        out_shape=tuple(
            pltpu.VMEM((sum(sizes[chunk] for chunk in wanted), columns), kind)
            for (_, wanted), kind in zip(jobs, kinds)
        ),
        compiler_params=room(12),
    )(*in_vmem(*(piece for pieces in chunks for piece in pieces), weight))


def join_kernel(one, other, out, *, low):
    rows = one[low : low + other.shape[0], :].astype(jnp.float32)
    out[...] = (rows + other[...].astype(jnp.float32)).astype(out.dtype)


def join(one, other, low):
    return pl.pallas_call(
        functools.partial(join_kernel, low=low),
        out_shape=pltpu.VMEM(other.shape, other.dtype),
        compiler_params=room(4),
        name="join",
    )(*in_vmem(one, other))


def finish_kernel(own, third, *refs):
    lates, lasts, out = refs[: len(refs) // 2], refs[len(refs) // 2 : -1], refs[-1]
    low = 0
    for late, last in zip(lates, lasts):
        rows = slice(low, low + late.shape[0])
        total = own[rows, :] + third[rows, :].astype(jnp.float32)
        total = total + late[...].astype(jnp.float32) + last[...].astype(jnp.float32)
        out[rows, :] = total.astype(out.dtype)
        low += late.shape[0]


def finish(own, third, lates, lasts):
    return pl.pallas_call(
        finish_kernel,
        out_shape=jax.ShapeDtypeStruct(own.shape, third.dtype),
        compiler_params=room(8),
        name="finish",
    )(*in_vmem(own, third, *lates, *lasts))


def exchanged(queries, key_vectors, value_vectors, out_weight):
    seq, ranks = lax.axis_size("seq"), lax.axis_size("head")
    chips = seq // 2
    heads = out_weight.shape[0] // VD // chips
    columns = out_weight.shape[1] // ranks
    length = queries.shape[0]
    cuts = (0, length // 2, length)
    bf16, f32 = jnp.bfloat16, jnp.float32

    packed = pack(queries, key_vectors, value_vectors, chips)
    mine = [packed[0]] + [swap(packed[turn], "seq", 2 * turn) for turn in range(1, chips)]
    partner = [swap(piece, "seq", 1) for piece in mine]
    results = attend(mine, partner, heads, cuts)
    weight = stage(out_weight)
    chunks = [[outs[0]] + [swap(outs[turn], "seq", 2 * turn) for turn in range(1, chips)] for outs in results]

    def hop(value, source, target):
        pairs = [(source, target), (ranks - 1 - source, ranks - 1 - target)]
        return lax.ppermute(value, "head", pairs)

    parts = range(len(chunks))
    to_first, to_second = [None, None], [None, None]
    (to_first[0],) = project(chunks[:1], weight, columns, ((0, (0,)),), (bf16,))
    (to_second[0],) = project(chunks[:1], weight, columns, ((1, (0,)),), (bf16,))
    (to_first[1],) = project(chunks[1:], weight, columns, ((0, (0,)),), (bf16,))
    to_second[1], to_third, own = project(
        chunks, weight, columns, ((1, (1,)), (2, (0, 1)), (3, (0, 1))), (bf16, bf16, f32)
    )
    first = [hop(to_first[part], 0, 1) for part in parts]
    second = [hop(to_second[part], 0, 1) for part in parts]
    third = hop(to_third, 0, 1)
    middle = [hop(join(to_first[part], first[part], 0), 1, 2) for part in parts]
    late = [hop(join(to_second[part], second[part], 0), 1, 2) for part in parts]
    last = [hop(join(to_third, middle[part], cuts[part]), 2, 3) for part in parts]
    return finish(own, third, late, last)


def gathered(queries, key_vectors, value_vectors, out_weight):
    heads_here = out_weight.shape[0] // VD
    length = queries.shape[0]
    here = lax.axis_index("seq")
    k_all = lax.all_gather(key_vectors, "seq", axis=0, tiled=True)
    v_all = lax.all_gather(value_vectors, "seq", axis=0, tiled=True)
    rows = here * length + jnp.arange(length, dtype=jnp.int32)
    causal = jnp.arange(k_all.shape[0], dtype=jnp.int32)[None, :] <= rows[:, None]
    results = []
    for head in range(heads_here):
        q = queries[:, head * KD : (head + 1) * KD]
        k = k_all[:, head * KD : (head + 1) * KD]
        v = v_all[:, head * VD : (head + 1) * VD]
        scores = jnp.einsum("bd,td->bt", q, k, preferred_element_type=jnp.float32) * KD ** (-0.5)
        weights = jnp.where(causal, 1.0 + scores + 0.5 * scores * scores, 0.0).astype(jnp.bfloat16)
        numer = jnp.dot(weights, v, preferred_element_type=jnp.float32)
        denom = jnp.sum(weights, axis=-1, dtype=jnp.float32)
        results.append((numer / denom[:, None]).astype(jnp.bfloat16))
    attention = jnp.concatenate(results, axis=1)
    partial = jnp.dot(attention, out_weight, preferred_element_type=jnp.float32)
    mixed = lax.psum_scatter(partial, "head", scatter_dimension=1, tiled=True)
    return mixed.astype(jnp.bfloat16)


def planned(seq, ranks, heads_here):
    chips = seq // 2
    paired = seq == 2 * chips and chips > 0 and chips & (chips - 1) == 0
    return paired and ranks == 4 and heads_here % chips == 0 and (heads_here // chips * KD) % 128 == 0


def per_device(queries, key_vectors, value_vectors, out_weight):
    if planned(lax.axis_size("seq"), lax.axis_size("head"), out_weight.shape[0] // VD):
        return exchanged(queries, key_vectors, value_vectors, out_weight)
    return gathered(queries, key_vectors, value_vectors, out_weight)


def solution(mesh):
    placed = (P("seq", "head"), P("seq", "head"), P("seq", "head"), P("head", None))
    step = jax.shard_map(
        per_device, mesh=mesh, in_specs=placed, out_specs=P("seq", "head"), check_vma=False
    )
    seq, ranks = mesh.shape["seq"], mesh.shape["head"]

    def whole(queries, key_vectors, value_vectors, out_weight):
        run = step
        if planned(seq, ranks, out_weight.shape[0] // ranks // VD):
            run = step
        return run(queries, key_vectors, value_vectors, out_weight)

    return whole
```

profile of v0, /device:TPU:0, one launch (start us, length us, event | category | flops | bytes accessed | tf_op | source)
XLA Modules:
  0.0 77.5 jit_solution(17022225844892004508)
XLA Ops:
  0.0 1.4 %pack.1 = (bf16[256,512]{1,0:T(8,128)(2,1)S(1)}, bf16[256,512]{1,0:T(8,128)(2,1)S(1)}, bf16[256,512]{1,0:T(8,128)(2,1)S(1)}, bf16[256,512]{1,0:T(8,128)(2,1)S(1)}) custom-call(bf16[256,512]{1,0:T(8,128)(2,1)} %q_ref.1, bf16[256,512]{1,0:T(8,128)(2,1)} %k_ref.1, bf16[256,1024]{1,0:T(8,128)(2,1)} %v_ref.1), custom_call_target="tpu_custom_call" | custom-call | tf_op jit(solution)/shard_map/pack/pallas_call | solution.py:61
  1.4 3.0 %collective-permute-start = (bf16[256,512]{1,0:T(8,128)(2,1)S(1)}, bf16[256,512]{1,0:T(8,128)(2,1)S(1)}, u32[]{:S(2)}, u32[]{:S(2)}) collective-permute-start(bf16[256,512]{1,0:T(8,128)(2,1)S(1)} %get-tuple-element.24), channel_id=1, source_target_pairs={{0,8},{4,12},{8,0},{12,4},{16,24},{20,28},{24,16},{28,20},{1,9},{5... | collective-permute-start | bytes 786440 | tf_op jit(solution)/shard_map/ppermute | solution.py:17
  4.5 1.5 %collective-permute-start.1 = (bf16[256,512]{1,0:T(8,128)(2,1)S(1)}, bf16[256,512]{1,0:T(8,128)(2,1)S(1)}, u32[]{:S(2)}, u32[]{:S(2)}) collective-permute-start(bf16[256,512]{1,0:T(8,128)(2,1)S(1)} %get-tuple-element.25), channel_id=1, source_target_pairs={{0,16},{4,20},{8,24},{12,28},{16,0},{20,4},{24,8},{28,12},{1,17},{... | collective-permute-start | bytes 786440 | tf_op jit(solution)/shard_map/ppermute | solution.py:17
  6.0 0.0 collective-permute-start.2
  6.0 0.0 collective-permute-start.3
  6.0 5.6 %collective-permute-done.refs_1_ = bf16[256,512]{1,0:T(8,128)(2,1)S(1)} collective-permute-done((bf16[256,512]{1,0:T(8,128)(2,1)S(1)}, bf16[256,512]{1,0:T(8,128)(2,1)S(1)}, u32[]{:S(2)}, u32[]{:S(2)}) %collective-permute-start) | collective-permute-done | bytes 262176 | tf_op jit(solution)/shard_map/ppermute | solution.py:17
  11.6 0.0 collective-permute-start.4
  11.6 6.2 %collective-permute-done.1.refs_2_ = bf16[256,512]{1,0:T(8,128)(2,1)S(1)} collective-permute-done((bf16[256,512]{1,0:T(8,128)(2,1)S(1)}, bf16[256,512]{1,0:T(8,128)(2,1)S(1)}, u32[]{:S(2)}, u32[]{:S(2)}) %collective-permute-start.1) | collective-permute-done | bytes 262176 | tf_op jit(solution)/shard_map/ppermute | solution.py:17
  17.8 0.0 collective-permute-start.5
  17.8 0.0 collective-permute-done.2.refs_3_
  17.8 0.5 collective-permute-start.6
  18.4 0.0 collective-permute-done.3.refs_4_
  18.4 0.0 collective-permute-done.4.refs_5_
  18.4 1.0 %collective-permute-done.5.refs_6_ = bf16[256,512]{1,0:T(8,128)(2,1)S(1)} collective-permute-done((bf16[256,512]{1,0:T(8,128)(2,1)S(1)}, bf16[256,512]{1,0:T(8,128)(2,1)S(1)}, u32[]{:S(2)}, u32[]{:S(2)}) %collective-permute-start.5) | collective-permute-done | bytes 262176 | tf_op jit(solution)/shard_map/ppermute | solution.py:17
  19.4 0.4 collective-permute-done.6.refs_7_
  19.8 2.2 %attend0.1 = (bf16[128,256]{1,0:T(8,128)(2,1)S(1)}, bf16[128,256]{1,0:T(8,128)(2,1)S(1)}, bf16[128,256]{1,0:T(8,128)(2,1)S(1)}, bf16[128,256]{1,0:T(8,128)(2,1)S...) custom-call(bf16[256,512]{1,0:T(8,128)(2,1)S(1)} %get-tuple-element.23.refs_0_, ...), custom_call_target="tpu_custom_call" | custom-call | tf_op jit(solution)/shard_map/attend0/pallas_call | solution.py:157
  22.0 0.9 %collective-permute-start.7 = (bf16[128,256]{1,0:T(8,128)(2,1)S(1)}, bf16[128,256]{1,0:T(8,128)(2,1)S(1)}, u32[]{:S(2)}, u32[]{:S(2)}) collective-permute-start(bf16[128,256]{1,0:T(8,128)(2,1)S(1)} %get-tuple-element.28), channel_id=1, source_target_pairs={{0,8},{4,12},{8,0},{12,4},{16,24},{20,28},{24,16},{28,20},{1,9},{5... | collective-permute-start | bytes 196616 | tf_op jit(solution)/shard_map/ppermute | solution.py:17
  22.9 1.2 %collective-permute-start.8 = (bf16[128,256]{1,0:T(8,128)(2,1)S(1)}, bf16[128,256]{1,0:T(8,128)(2,1)S(1)}, u32[]{:S(2)}, u32[]{:S(2)}) collective-permute-start(bf16[128,256]{1,0:T(8,128)(2,1)S(1)} %get-tuple-element.29), channel_id=1, source_target_pairs={{0,16},{4,20},{8,24},{12,28},{16,0},{20,4},{24,8},{28,12},{1,17},{... | collective-permute-start | bytes 196616 | tf_op jit(solution)/shard_map/ppermute | solution.py:17
  24.1 1.4 %collective-permute-start.9 = (bf16[128,256]{1,0:T(8,128)(2,1)S(1)}, bf16[128,256]{1,0:T(8,128)(2,1)S(1)}, u32[]{:S(2)}, u32[]{:S(2)}) collective-permute-start(bf16[128,256]{1,0:T(8,128)(2,1)S(1)} %get-tuple-element.30), channel_id=1, source_target_pairs={{0,24},{4,28},{8,16},{12,20},{16,8},{20,12},{24,0},{28,4},{1,25},{... | collective-permute-start | bytes 196616 | tf_op jit(solution)/shard_map/ppermute | solution.py:17
  25.5 1.9 %shard_map.46 = (bf16[128,256]{1,0:T(8,128)(2,1)S(1)}, bf16[128,256]{1,0:T(8,128)(2,1)S(1)}, bf16[128,256]{1,0:T(8,128)(2,1)S(1)}, bf16[128,256]{1,0:T(8,128)(2,1)S(1)}) custom-call(bf16[1024,128]{1,0:T(8,128)(2,1)S(1)} %get-tuple-element.31.q_all, bf16[2048,128]{1,0:T(8,128)(2,1)S(1)} %get-tuple-element.32.k_all, bf16[2048,512]{1,0:T(8,128)(2,1)S(1)} %get-tuple-element.33.v_all), custom_call_target="tpu_custom_call" | custom-call | tf_op jit(solution)/shard_map/pallas_call | solution.py:172
  27.4 0.9 %collective-permute-start.10 = (bf16[128,256]{1,0:T(8,128)(2,1)S(1)}, bf16[128,256]{1,0:T(8,128)(2,1)S(1)}, u32[]{:S(2)}, u32[]{:S(2)}) collective-permute-start(bf16[128,256]{1,0:T(8,128)(2,1)S(1)} %get-tuple-element.35), channel_id=1, source_target_pairs={{0,8},{4,12},{8,0},{12,4},{16,24},{20,28},{24,16},{28,20},{1,9},{5... | collective-permute-start | bytes 196616 | tf_op jit(solution)/shard_map/ppermute | solution.py:17
  28.4 1.2 %collective-permute-start.11 = (bf16[128,256]{1,0:T(8,128)(2,1)S(1)}, bf16[128,256]{1,0:T(8,128)(2,1)S(1)}, u32[]{:S(2)}, u32[]{:S(2)}) collective-permute-start(bf16[128,256]{1,0:T(8,128)(2,1)S(1)} %get-tuple-element.36), channel_id=1, source_target_pairs={{0,16},{4,20},{8,24},{12,28},{16,0},{20,4},{24,8},{28,12},{1,17},{... | collective-permute-start | bytes 196616 | tf_op jit(solution)/shard_map/ppermute | solution.py:17
  29.6 0.0 collective-permute-done.7.refs_1_
  29.6 1.4 %collective-permute-start.12 = (bf16[128,256]{1,0:T(8,128)(2,1)S(1)}, bf16[128,256]{1,0:T(8,128)(2,1)S(1)}, u32[]{:S(2)}, u32[]{:S(2)}) collective-permute-start(bf16[128,256]{1,0:T(8,128)(2,1)S(1)} %get-tuple-element.37), channel_id=1, source_target_pairs={{0,24},{4,28},{8,16},{12,20},{16,8},{20,12},{24,0},{28,4},{1,25},{... | collective-permute-start | bytes 196616 | tf_op jit(solution)/shard_map/ppermute | solution.py:17
  31.0 3.4 %stage.1.refs_8_.refs_4_ = bf16[1024,4096]{1,0:T(8,128)(2,1)S(1)} custom-call(bf16[1024,4096]{1,0:T(8,128)(2,1)} %w_ref.1), custom_call_target="tpu_custom_call" | custom-call | tf_op jit(solution)/shard_map/stage/pallas_call | solution.py:78
  34.4 0.0 collective-permute-done.8.refs_2_
  34.4 0.0 collective-permute-done.9.refs_3_
  34.4 0.5 shard_map.49.one
  34.9 3.5 %collective-permute-start.18 = (bf16[128,1024]{1,0:T(8,128)(2,1)S(1)}, bf16[128,1024]{1,0:T(8,128)(2,1)S(1)}, u32[]{:S(2)}, u32[]{:S(2)}) collective-permute-start(bf16[128,1024]{1,0:T(8,128)(2,1)S(1)} %shard_map.49.one), channel_id=1, source_target_pairs={{0,1},{3,2},{4,5},{7,6},{8,9},{11,10},{12,13},{15,14},{16,17},{19,... | collective-permute-start | bytes 786440 | tf_op jit(solution)/shard_map/ppermute | solution.py:274
  38.4 0.0 collective-permute-done.10.refs_5_.refs_1_
  38.4 0.0 collective-permute-done.11.refs_6_.refs_2_
  38.4 0.0 collective-permute-done.12.refs_7_.refs_3_
  38.4 0.5 shard_map.50.one
  38.9 1.3 %collective-permute-start.21 = (bf16[128,1024]{1,0:T(8,128)(2,1)S(1)}, bf16[128,1024]{1,0:T(8,128)(2,1)S(1)}, u32[]{:S(2)}, u32[]{:S(2)}) collective-permute-start(bf16[128,1024]{1,0:T(8,128)(2,1)S(1)} %shard_map.50.one), channel_id=1, source_target_pairs={{0,1},{3,2},{4,5},{7,6},{8,9},{11,10},{12,13},{15,14},{16,17},{19,... | collective-permute-start | bytes 786440 | tf_op jit(solution)/shard_map/ppermute | solution.py:274
  40.2 1.5 %shard_map.47 = (bf16[128,1024]{1,0:T(8,128)(2,1)S(1)}, bf16[256,1024]{1,0:T(8,128)(2,1)S(1)}, f32[256,1024]{1,0:T(8,128)S(1)}) custom-call(bf16[128,256]{1,0:T(8,128)(2,1)S(1)} %get-tuple-element.27.refs_0_, bf16[128,256]{1,0:T(8,128)(2,1)S(1)} %collective-permute-done.7.refs_1_, bf16[128,256]{1,0:T(8,128)(2,1)S(1)} %collective-permute-done.8.refs_2_, ...), custom_call_target="tpu_custom_call" | custom-call | tf_op jit(solution)/shard_map/pallas_call | solution.py:212
  41.8 1.3 %collective-permute-start.16 = (bf16[128,1024]{1,0:T(8,128)(2,1)S(1)}, bf16[128,1024]{1,0:T(8,128)(2,1)S(1)}, u32[]{:S(2)}, u32[]{:S(2)}) collective-permute-start(bf16[128,1024]{1,0:T(8,128)(2,1)S(1)} %get-tuple-element.40.one), channel_id=1, source_target_pairs={{0,1},{3,2},{4,5},{7,6},{8,9},{11,10},{12,13},{15,14},{16,17},{19,... | collective-permute-start | bytes 786440 | tf_op jit(solution)/shard_map/ppermute | solution.py:274
  43.1 0.5 shard_map.48.one
  43.5 1.3 %collective-permute-start.14 = (bf16[128,1024]{1,0:T(8,128)(2,1)S(1)}, bf16[128,1024]{1,0:T(8,128)(2,1)S(1)}, u32[]{:S(2)}, u32[]{:S(2)}) collective-permute-start(bf16[128,1024]{1,0:T(8,128)(2,1)S(1)} %shard_map.48.one), channel_id=1, source_target_pairs={{0,1},{3,2},{4,5},{7,6},{8,9},{11,10},{12,13},{15,14},{16,17},{19,... | collective-permute-start | bytes 786440 | tf_op jit(solution)/shard_map/ppermute | solution.py:274
  44.8 1.3 %collective-permute-start.13 = (bf16[256,1024]{1,0:T(8,128)(2,1)S(1)}, bf16[256,1024]{1,0:T(8,128)(2,1)S(1)}, u32[]{:S(2)}, u32[]{:S(2)}) collective-permute-start(bf16[256,1024]{1,0:T(8,128)(2,1)S(1)} %get-tuple-element.39.one), channel_id=1, source_target_pairs={{0,1},{3,2},{4,5},{7,6},{8,9},{11,10},{12,13},{15,14},{16,17},{19,... | collective-permute-start | bytes 1572872 | tf_op jit(solution)/shard_map/ppermute | solution.py:274
  46.2 0.0 collective-permute-done.18.other
  46.2 0.1 join.8
  46.3 0.7 collective-permute-start.19
  46.9 3.7 %collective-permute-done.21.other = bf16[128,1024]{1,0:T(8,128)(2,1)S(1)} collective-permute-done((bf16[128,1024]{1,0:T(8,128)(2,1)S(1)}, bf16[128,1024]{1,0:T(8,128)(2,1)S(1)}, u32[]{:S(2)}, u32[]{:S(2)}) %collective-permute-start.21) | collective-permute-done | bytes 262176 | tf_op jit(solution)/shard_map/ppermute | solution.py:274
  50.7 0.1 join.10
  50.7 0.7 collective-permute-start.22
  51.4 4.9 %collective-permute-done.16.other = bf16[128,1024]{1,0:T(8,128)(2,1)S(1)} collective-permute-done((bf16[128,1024]{1,0:T(8,128)(2,1)S(1)}, bf16[128,1024]{1,0:T(8,128)(2,1)S(1)}, u32[]{:S(2)}, u32[]{:S(2)}) %collective-permute-start.16) | collective-permute-done | bytes 262176 | tf_op jit(solution)/shard_map/ppermute | solution.py:274
  56.3 0.1 join.7
  56.3 0.7 collective-permute-start.17
  57.0 4.9 %collective-permute-done.14.other = bf16[128,1024]{1,0:T(8,128)(2,1)S(1)} collective-permute-done((bf16[128,1024]{1,0:T(8,128)(2,1)S(1)}, bf16[128,1024]{1,0:T(8,128)(2,1)S(1)}, u32[]{:S(2)}, u32[]{:S(2)}) %collective-permute-start.14) | collective-permute-done | bytes 262176 | tf_op jit(solution)/shard_map/ppermute | solution.py:274
  61.9 0.1 join.6
  62.0 0.7 collective-permute-start.15
  62.6 0.0 collective-permute-done.19.other
  62.7 0.1 join.9
  62.7 1.3 %collective-permute-start.20 = (bf16[128,1024]{1,0:T(8,128)(2,1)S(1)}, bf16[128,1024]{1,0:T(8,128)(2,1)S(1)}, u32[]{:S(2)}, u32[]{:S(2)}) collective-permute-start(bf16[128,1024]{1,0:T(8,128)(2,1)S(1)} %join.9), channel_id=1, source_target_pairs={{2,3},{1,0},{6,7},{5,4},{10,11},{9,8},{14,15},{13,12},{18,19},{17,... | collective-permute-start | bytes 786440 | tf_op jit(solution)/shard_map/ppermute | solution.py:274
  64.0 0.0 collective-permute-done.22.other
  64.0 0.1 join.11
  64.1 1.3 %collective-permute-start.23 = (bf16[128,1024]{1,0:T(8,128)(2,1)S(1)}, bf16[128,1024]{1,0:T(8,128)(2,1)S(1)}, u32[]{:S(2)}, u32[]{:S(2)}) collective-permute-start(bf16[128,1024]{1,0:T(8,128)(2,1)S(1)} %join.11), channel_id=1, source_target_pairs={{2,3},{1,0},{6,7},{5,4},{10,11},{9,8},{14,15},{13,12},{18,19},{17,... | collective-permute-start | bytes 786440 | tf_op jit(solution)/shard_map/ppermute | solution.py:274
  65.4 5.2 %collective-permute-done.13.third = bf16[256,1024]{1,0:T(8,128)(2,1)S(1)} collective-permute-done((bf16[256,1024]{1,0:T(8,128)(2,1)S(1)}, bf16[256,1024]{1,0:T(8,128)(2,1)S(1)}, u32[]{:S(2)}, u32[]{:S(2)}) %collective-permute-start.13) | collective-permute-done | bytes 524320 | tf_op jit(solution)/shard_map/ppermute | solution.py:274
  70.6 0.0 collective-permute-done.17.refs_1_
  70.6 0.0 collective-permute-done.15.refs_0_
  70.6 3.0 %collective-permute-done.20.refs_2_ = bf16[128,1024]{1,0:T(8,128)(2,1)S(1)} collective-permute-done((bf16[128,1024]{1,0:T(8,128)(2,1)S(1)}, bf16[128,1024]{1,0:T(8,128)(2,1)S(1)}, u32[]{:S(2)}, u32[]{:S(2)}) %collective-permute-start.20) | collective-permute-done | bytes 262176 | tf_op jit(solution)/shard_map/ppermute | solution.py:274
  73.6 2.8 %collective-permute-done.23.refs_3_ = bf16[128,1024]{1,0:T(8,128)(2,1)S(1)} collective-permute-done((bf16[128,1024]{1,0:T(8,128)(2,1)S(1)}, bf16[128,1024]{1,0:T(8,128)(2,1)S(1)}, u32[]{:S(2)}, u32[]{:S(2)}) %collective-permute-start.23) | collective-permute-done | bytes 262176 | tf_op jit(solution)/shard_map/ppermute | solution.py:274
  76.5 1.0 %finish.1 = bf16[256,1024]{1,0:T(8,128)(2,1)} custom-call(f32[256,1024]{1,0:T(8,128)S(1)} %get-tuple-element.38.own, bf16[256,1024]{1,0:T(8,128)(2,1)S(1)} %collective-permute-done.13.third, bf16[128,1024]{1,0:T(8,128)(2,1)S(1)} %collective-permute-done.15.refs_0_, bf16[128,1024]{1,0:T(8,128)(2,1)S(1)} %collective-permute-done.17.refs_1_, ...), custom_call_target="tpu_custom_call" | custom-call | tf_op jit(solution)/shard_map/finish/pallas_call | solution.py:248
Async XLA Ops:
  1.4 10.2 %collective-permute-start = (bf16[256,512]{1,0:T(8,128)(2,1)S(1)}, bf16[256,512]{1,0:T(8,128)(2,1)S(1)}, u32[]{:S(2)}, u32[]{:S(2)}) collective-permute-start(bf16[256,512]{1,0:T(8,128)(2,1)S(1)} %get-tuple-element.24), channel_id=1, source_target_pairs={{0,8},{4,12},{8,0},{12,4},{16,24},{20,28},{24,16},{28,20},{1,9},{5... | collective-permute-start | bytes 786440 | tf_op jit(solution)/shard_map/ppermute | solution.py:17
  4.5 13.4 %collective-permute-start.1 = (bf16[256,512]{1,0:T(8,128)(2,1)S(1)}, bf16[256,512]{1,0:T(8,128)(2,1)S(1)}, u32[]{:S(2)}, u32[]{:S(2)}) collective-permute-start(bf16[256,512]{1,0:T(8,128)(2,1)S(1)} %get-tuple-element.25), channel_id=1, source_target_pairs={{0,16},{4,20},{8,24},{12,28},{16,0},{20,4},{24,8},{28,12},{1,17},{... | collective-permute-start | bytes 786440 | tf_op jit(solution)/shard_map/ppermute | solution.py:17
  6.0 11.9 %collective-permute-start.2 = (bf16[256,512]{1,0:T(8,128)(2,1)S(1)}, bf16[256,512]{1,0:T(8,128)(2,1)S(1)}, u32[]{:S(2)}, u32[]{:S(2)}) collective-permute-start(bf16[256,512]{1,0:T(8,128)(2,1)S(1)} %get-tuple-element.26), channel_id=1, source_target_pairs={{0,24},{4,28},{8,16},{12,20},{16,8},{20,12},{24,0},{28,4},{1,25},{... | collective-permute-start | bytes 786440 | tf_op jit(solution)/shard_map/ppermute | solution.py:17
  6.0 12.4 %collective-permute-start.3 = (bf16[256,512]{1,0:T(8,128)(2,1)S(1)}, bf16[256,512]{1,0:T(8,128)(2,1)S(1)}, u32[]{:S(2)}, u32[]{:S(2)}) collective-permute-start(bf16[256,512]{1,0:T(8,128)(2,1)S(1)} %get-tuple-element.23.refs_0_), channel_id=1, source_target_pairs={{0,4},{4,0},{8,12},{12,8},{16,20},{20,16},{24,28},{28,24},{1,5},{5... | collective-permute-start | bytes 786440 | tf_op jit(solution)/shard_map/ppermute | solution.py:17
  11.6 6.7 %collective-permute-start.4 = (bf16[256,512]{1,0:T(8,128)(2,1)S(1)}, bf16[256,512]{1,0:T(8,128)(2,1)S(1)}, u32[]{:S(2)}, u32[]{:S(2)}) collective-permute-start(bf16[256,512]{1,0:T(8,128)(2,1)S(1)} %collective-permute-done.refs_1_), channel_id=1, source_target_pairs={{0,4},{4,0},{8,12},{12,8},{16,20},{20,16},{24,28},{28,24},{1,5},{5... | collective-permute-start | bytes 786440 | tf_op jit(solution)/shard_map/ppermute | solution.py:17
  17.8 1.5 %collective-permute-start.5 = (bf16[256,512]{1,0:T(8,128)(2,1)S(1)}, bf16[256,512]{1,0:T(8,128)(2,1)S(1)}, u32[]{:S(2)}, u32[]{:S(2)}) collective-permute-start(bf16[256,512]{1,0:T(8,128)(2,1)S(1)} %collective-permute-done.1.refs_2_), channel_id=1, source_target_pairs={{0,4},{4,0},{8,12},{12,8},{16,20},{20,16},{24,28},{28,24},{1,5},{5... | collective-permute-start | bytes 786440 | tf_op jit(solution)/shard_map/ppermute | solution.py:17
  17.8 1.9 %collective-permute-start.6 = (bf16[256,512]{1,0:T(8,128)(2,1)S(1)}, bf16[256,512]{1,0:T(8,128)(2,1)S(1)}, u32[]{:S(2)}, u32[]{:S(2)}) collective-permute-start(bf16[256,512]{1,0:T(8,128)(2,1)S(1)} %collective-permute-done.2.refs_3_), channel_id=1, source_target_pairs={{0,4},{4,0},{8,12},{12,8},{16,20},{20,16},{24,28},{28,24},{1,5},{5... | collective-permute-start | bytes 786440 | tf_op jit(solution)/shard_map/ppermute | solution.py:17
  22.0 7.6 %collective-permute-start.7 = (bf16[128,256]{1,0:T(8,128)(2,1)S(1)}, bf16[128,256]{1,0:T(8,128)(2,1)S(1)}, u32[]{:S(2)}, u32[]{:S(2)}) collective-permute-start(bf16[128,256]{1,0:T(8,128)(2,1)S(1)} %get-tuple-element.28), channel_id=1, source_target_pairs={{0,8},{4,12},{8,0},{12,4},{16,24},{20,28},{24,16},{28,20},{1,9},{5... | collective-permute-start | bytes 196616 | tf_op jit(solution)/shard_map/ppermute | solution.py:17
  22.9 11.5 %collective-permute-start.8 = (bf16[128,256]{1,0:T(8,128)(2,1)S(1)}, bf16[128,256]{1,0:T(8,128)(2,1)S(1)}, u32[]{:S(2)}, u32[]{:S(2)}) collective-permute-start(bf16[128,256]{1,0:T(8,128)(2,1)S(1)} %get-tuple-element.29), channel_id=1, source_target_pairs={{0,16},{4,20},{8,24},{12,28},{16,0},{20,4},{24,8},{28,12},{1,17},{... | collective-permute-start | bytes 196616 | tf_op jit(solution)/shard_map/ppermute | solution.py:17
  24.1 10.3 %collective-permute-start.9 = (bf16[128,256]{1,0:T(8,128)(2,1)S(1)}, bf16[128,256]{1,0:T(8,128)(2,1)S(1)}, u32[]{:S(2)}, u32[]{:S(2)}) collective-permute-start(bf16[128,256]{1,0:T(8,128)(2,1)S(1)} %get-tuple-element.30), channel_id=1, source_target_pairs={{0,24},{4,28},{8,16},{12,20},{16,8},{20,12},{24,0},{28,4},{1,25},{... | collective-permute-start | bytes 196616 | tf_op jit(solution)/shard_map/ppermute | solution.py:17
  27.4 10.9 %collective-permute-start.10 = (bf16[128,256]{1,0:T(8,128)(2,1)S(1)}, bf16[128,256]{1,0:T(8,128)(2,1)S(1)}, u32[]{:S(2)}, u32[]{:S(2)}) collective-permute-start(bf16[128,256]{1,0:T(8,128)(2,1)S(1)} %get-tuple-element.35), channel_id=1, source_target_pairs={{0,8},{4,12},{8,0},{12,4},{16,24},{20,28},{24,16},{28,20},{1,9},{5... | collective-permute-start | bytes 196616 | tf_op jit(solution)/shard_map/ppermute | solution.py:17
  28.4 10.0 %collective-permute-start.11 = (bf16[128,256]{1,0:T(8,128)(2,1)S(1)}, bf16[128,256]{1,0:T(8,128)(2,1)S(1)}, u32[]{:S(2)}, u32[]{:S(2)}) collective-permute-start(bf16[128,256]{1,0:T(8,128)(2,1)S(1)} %get-tuple-element.36), channel_id=1, source_target_pairs={{0,16},{4,20},{8,24},{12,28},{16,0},{20,4},{24,8},{28,12},{1,17},{... | collective-permute-start | bytes 196616 | tf_op jit(solution)/shard_map/ppermute | solution.py:17
  29.6 8.8 %collective-permute-start.12 = (bf16[128,256]{1,0:T(8,128)(2,1)S(1)}, bf16[128,256]{1,0:T(8,128)(2,1)S(1)}, u32[]{:S(2)}, u32[]{:S(2)}) collective-permute-start(bf16[128,256]{1,0:T(8,128)(2,1)S(1)} %get-tuple-element.37), channel_id=1, source_target_pairs={{0,24},{4,28},{8,16},{12,20},{16,8},{20,12},{24,0},{28,4},{1,25},{... | collective-permute-start | bytes 196616 | tf_op jit(solution)/shard_map/ppermute | solution.py:17
  34.9 11.3 %collective-permute-start.18 = (bf16[128,1024]{1,0:T(8,128)(2,1)S(1)}, bf16[128,1024]{1,0:T(8,128)(2,1)S(1)}, u32[]{:S(2)}, u32[]{:S(2)}) collective-permute-start(bf16[128,1024]{1,0:T(8,128)(2,1)S(1)} %shard_map.49.one), channel_id=1, source_target_pairs={{0,1},{3,2},{4,5},{7,6},{8,9},{11,10},{12,13},{15,14},{16,17},{19,... | collective-permute-start | bytes 786440 | tf_op jit(solution)/shard_map/ppermute | solution.py:274
  38.9 11.8 %collective-permute-start.21 = (bf16[128,1024]{1,0:T(8,128)(2,1)S(1)}, bf16[128,1024]{1,0:T(8,128)(2,1)S(1)}, u32[]{:S(2)}, u32[]{:S(2)}) collective-permute-start(bf16[128,1024]{1,0:T(8,128)(2,1)S(1)} %shard_map.50.one), channel_id=1, source_target_pairs={{0,1},{3,2},{4,5},{7,6},{8,9},{11,10},{12,13},{15,14},{16,17},{19,... | collective-permute-start | bytes 786440 | tf_op jit(solution)/shard_map/ppermute | solution.py:274
  41.8 14.5 %collective-permute-start.16 = (bf16[128,1024]{1,0:T(8,128)(2,1)S(1)}, bf16[128,1024]{1,0:T(8,128)(2,1)S(1)}, u32[]{:S(2)}, u32[]{:S(2)}) collective-permute-start(bf16[128,1024]{1,0:T(8,128)(2,1)S(1)} %get-tuple-element.40.one), channel_id=1, source_target_pairs={{0,1},{3,2},{4,5},{7,6},{8,9},{11,10},{12,13},{15,14},{16,17},{19,... | collective-permute-start | bytes 786440 | tf_op jit(solution)/shard_map/ppermute | solution.py:274
  43.5 18.4 %collective-permute-start.14 = (bf16[128,1024]{1,0:T(8,128)(2,1)S(1)}, bf16[128,1024]{1,0:T(8,128)(2,1)S(1)}, u32[]{:S(2)}, u32[]{:S(2)}) collective-permute-start(bf16[128,1024]{1,0:T(8,128)(2,1)S(1)} %shard_map.48.one), channel_id=1, source_target_pairs={{0,1},{3,2},{4,5},{7,6},{8,9},{11,10},{12,13},{15,14},{16,17},{19,... | collective-permute-start | bytes 786440 | tf_op jit(solution)/shard_map/ppermute | solution.py:274
  44.8 25.8 %collective-permute-start.13 = (bf16[256,1024]{1,0:T(8,128)(2,1)S(1)}, bf16[256,1024]{1,0:T(8,128)(2,1)S(1)}, u32[]{:S(2)}, u32[]{:S(2)}) collective-permute-start(bf16[256,1024]{1,0:T(8,128)(2,1)S(1)} %get-tuple-element.39.one), channel_id=1, source_target_pairs={{0,1},{3,2},{4,5},{7,6},{8,9},{11,10},{12,13},{15,14},{16,17},{19,... | collective-permute-start | bytes 1572872 | tf_op jit(solution)/shard_map/ppermute | solution.py:274
  46.3 16.4 %collective-permute-start.19 = (bf16[128,1024]{1,0:T(8,128)(2,1)S(1)}, bf16[128,1024]{1,0:T(8,128)(2,1)S(1)}, u32[]{:S(2)}, u32[]{:S(2)}) collective-permute-start(bf16[128,1024]{1,0:T(8,128)(2,1)S(1)} %join.8), channel_id=1, source_target_pairs={{1,2},{2,1},{5,6},{6,5},{9,10},{10,9},{13,14},{14,13},{17,18},{18,... | collective-permute-start | bytes 786440 | tf_op jit(solution)/shard_map/ppermute | solution.py:274
  50.7 13.3 %collective-permute-start.22 = (bf16[128,1024]{1,0:T(8,128)(2,1)S(1)}, bf16[128,1024]{1,0:T(8,128)(2,1)S(1)}, u32[]{:S(2)}, u32[]{:S(2)}) collective-permute-start(bf16[128,1024]{1,0:T(8,128)(2,1)S(1)} %join.10), channel_id=1, source_target_pairs={{1,2},{2,1},{5,6},{6,5},{9,10},{10,9},{13,14},{14,13},{17,18},{18,... | collective-permute-start | bytes 786440 | tf_op jit(solution)/shard_map/ppermute | solution.py:274
  56.3 14.3 %collective-permute-start.17 = (bf16[128,1024]{1,0:T(8,128)(2,1)S(1)}, bf16[128,1024]{1,0:T(8,128)(2,1)S(1)}, u32[]{:S(2)}, u32[]{:S(2)}) collective-permute-start(bf16[128,1024]{1,0:T(8,128)(2,1)S(1)} %join.7), channel_id=1, source_target_pairs={{1,2},{2,1},{5,6},{6,5},{9,10},{10,9},{13,14},{14,13},{17,18},{18,... | collective-permute-start | bytes 786440 | tf_op jit(solution)/shard_map/ppermute | solution.py:274
  62.0 8.7 %collective-permute-start.15 = (bf16[128,1024]{1,0:T(8,128)(2,1)S(1)}, bf16[128,1024]{1,0:T(8,128)(2,1)S(1)}, u32[]{:S(2)}, u32[]{:S(2)}) collective-permute-start(bf16[128,1024]{1,0:T(8,128)(2,1)S(1)} %join.6), channel_id=1, source_target_pairs={{1,2},{2,1},{5,6},{6,5},{9,10},{10,9},{13,14},{14,13},{17,18},{18,... | collective-permute-start | bytes 786440 | tf_op jit(solution)/shard_map/ppermute | solution.py:274
  62.7 10.9 %collective-permute-start.20 = (bf16[128,1024]{1,0:T(8,128)(2,1)S(1)}, bf16[128,1024]{1,0:T(8,128)(2,1)S(1)}, u32[]{:S(2)}, u32[]{:S(2)}) collective-permute-start(bf16[128,1024]{1,0:T(8,128)(2,1)S(1)} %join.9), channel_id=1, source_target_pairs={{2,3},{1,0},{6,7},{5,4},{10,11},{9,8},{14,15},{13,12},{18,19},{17,... | collective-permute-start | bytes 786440 | tf_op jit(solution)/shard_map/ppermute | solution.py:274
  64.1 12.3 %collective-permute-start.23 = (bf16[128,1024]{1,0:T(8,128)(2,1)S(1)}, bf16[128,1024]{1,0:T(8,128)(2,1)S(1)}, u32[]{:S(2)}, u32[]{:S(2)}) collective-permute-start(bf16[128,1024]{1,0:T(8,128)(2,1)S(1)} %join.11), channel_id=1, source_target_pairs={{2,3},{1,0},{6,7},{5,4},{10,11},{9,8},{14,15},{13,12},{18,19},{17,... | collective-permute-start | bytes 786440 | tf_op jit(solution)/shard_map/ppermute | solution.py:274
where the time goes:
time: 77.8 us; the launch traced here: 77.5 us
  waiting for transfers between devices  37.8 us (49%)
  starting transfers between devices  26.2 us (34%)
  Pallas kernels  13.3 us (17%)
    ppermute x11, waiting for transfers between devices, hop(): return lax.ppermute(value, 'head', pairs)  24.5 us
    ppermute x11, starting transfers between devices, hop(): return lax.ppermute(value, 'head', pairs)  14 us
    ppermute x13, waiting for transfers between devices, swap(): return lax.ppermute(value, axis, [(i, i ^ bits) for i in range(count)])  13.2 us
    ppermute x13, starting transfers between devices, swap(): return lax.ppermute(value, axis, [(i, i ^ bits) for i in range(count)])  12.2 us
    pallas_call x1, Pallas kernels, stage(): pl.pallas_call(stage_kernel, out_shape=pltpu.VMEM(weight.shape, weight.dt...  3.39 us
    pallas_call x4, Pallas kernels, project(): pl.pallas_call(functools.partial(project_kernel, chips=len(chunks[0]), ch...  2.94 us
    pallas_call x1, Pallas kernels, attend(): pl.pallas_call(functools.partial(attend_first_kernel, chips=chips, heads=...  2.23 us
    pallas_call x1, Pallas kernels, attend(): pl.pallas_call(functools.partial(attend_later_kernel, chips=chips, heads=...  1.89 us
  transfers between devices with their start and end apart: 24, of which 10 were waited for; matrix products, arithmetic and copies ran while one was open for 0% of the time, Pallas kernels for 11%

commit v1 on v0

--- a/solution.py
+++ b/solution.py
@@ -34,35 +34,51 @@
     return here >> 1, here & 1
 
 
-def pack_kernel(q_ref, k_ref, v_ref, *refs):
-    outs, arrived = refs[:-1], refs[-1]
-    wide_k = outs[0].shape[1] // 4
+def stacks(count, tiles):
+    high = -(-count // (16 * tiles)) * 16
+    return high, [(at, min(high, count - at)) for at in range(0, count, high)]
+
+
+def pack_kernel(q_ref, k_ref, v_ref, *refs, first):
+    half = (len(refs) - 1) // 2
+    outs, laters, arrived = refs[:half], refs[half:-1], refs[-1]
+    length, wide_k = q_ref.shape[0], laters[0].shape[1]
+    _, rows_of = stacks(first, outs[0].shape[1] // wide_k)
     here, _ = seat()
     copies = []
-    for turn in (*range(1, len(outs)), 0):
-        at = 0
-        for source, wide in ((q_ref, wide_k), (k_ref, wide_k), (v_ref, 2 * wide_k)):
-            columns = pl.ds(pl.multiple_of((here ^ turn) * wide, wide), wide)
-            copies.append(
-                pltpu.make_async_copy(
-                    source.at[:, columns], outs[turn].at[:, at : at + wide], arrived.at[len(copies)]
-                )
+
+    def copy(source, target):
+        copies.append(pltpu.make_async_copy(source, target, arrived.at[len(copies)]))
+        copies[-1].start()
+
+    for turn in (*range(1, half), 0):
+        out, later = outs[turn], laters[turn]
+        narrow = pl.ds(pl.multiple_of((here ^ turn) * wide_k, wide_k), wide_k)
+        wide = pl.ds(pl.multiple_of((here ^ turn) * 2 * wide_k, 2 * wide_k), 2 * wide_k)
+        copy(k_ref.at[:, narrow], out.at[:length, :wide_k])
+        copy(v_ref.at[:, wide], out.at[:length, wide_k:])
+        for tile, (at, size) in enumerate(rows_of):
+            copy(
+                q_ref.at[at : at + size, narrow],
+                out.at[length : length + size, tile * wide_k : (tile + 1) * wide_k],
             )
-            at += wide
-    for copy in copies:
-        copy.start()
-    for copy in copies:
-        copy.wait()
-
-
-def pack(queries, keys, values, chips):
-    length, width = queries.shape
-    each = pltpu.VMEM((length, 4 * width // chips), queries.dtype)
-    return pl.pallas_call(
-        pack_kernel,
-        out_shape=(each,) * chips,
+        copy(q_ref.at[first:, narrow], later)
+    for each in copies:
+        each.wait()
+
+
+def pack(queries, keys, values, chips, first):
+    (length, width), kind = queries.shape, queries.dtype
+    wide_k = width // chips
+    high, rows_of = stacks(first, 3)
+    return pl.pallas_call(
+        functools.partial(pack_kernel, first=first),
+        out_shape=(
+            *(pltpu.VMEM((length + high, 3 * wide_k), kind),) * chips,
+            *(pltpu.VMEM((length - first, wide_k), kind),) * chips,
+        ),
         in_specs=[pl.BlockSpec(memory_space=pltpu.HBM)] * 3,
-        scratch_shapes=[pltpu.SemaphoreType.DMA((3 * chips,))],
+        scratch_shapes=[pltpu.SemaphoreType.DMA(((3 + len(rows_of)) * chips,))],
         compiler_params=room(8),
         name="pack",
     )(*in_hbm(queries, keys, values))
@@ -85,15 +101,14 @@
     )(*in_hbm(weight))
 
 
-def attend_rows(q_all, k_all, v_all, o_all, rows_from, core, chips, heads):
+def attend_rows(q_part, k_all, v_all, o_all, rows_from, core, chips, heads):
     length, wide_k = k_all.shape[0] // (2 * chips), heads * KD
     count = o_all.shape[0] // chips
     row = lax.broadcasted_iota(jnp.int32, (count, 2 * length), 0) + (core * length + rows_from)
     seen = lax.broadcasted_iota(jnp.int32, (count, 2 * length), 1) <= row
     lane = lax.broadcasted_iota(jnp.int32, (count, wide_k), 1) // KD
     for index in range(chips):
-        at = index * length + rows_from
-        q = q_all[at : at + count, :] * jnp.bfloat16(KD ** (-0.5))
+        q = q_part[index * count : (index + 1) * count, :] * jnp.bfloat16(KD ** (-0.5))
         for head in range(heads):
             own = jnp.where(lane == head, q, jnp.bfloat16(0))
             columns = slice(2 * head * VD, (2 * head + 2) * VD)
@@ -124,59 +139,66 @@
 
 def attend_first_kernel(*refs, chips, heads):
     mine, partner = refs[:chips], refs[chips : 2 * chips]
-    outs, (q_all, k_all, v_all) = refs[2 * chips : 3 * chips], refs[3 * chips : 3 * chips + 3]
-    o_all = refs[-1]
-    length = mine[0].shape[0]
+    outs, (k_all, v_all) = refs[2 * chips : 3 * chips], refs[3 * chips : 3 * chips + 2]
+    q_part, o_all = refs[-2:]
     wide_k = heads * KD
+    length, count = k_all.shape[0] // (2 * chips), q_part.shape[0] // chips
+    _, rows_of = stacks(count, mine[0].shape[1] // wide_k)
     chip, core = seat()
     ones = jnp.ones((length, VD), jnp.bfloat16)
     for turn in range(chips):
         there = chip ^ turn
-        q_all[pl.ds(pl.multiple_of(there * length, length), length), :] = mine[turn][:, :wide_k]
+        for tile, (at, size) in enumerate(rows_of):
+            q_part[pl.ds(pl.multiple_of(there * count + at, 16), size), :] = mine[turn][
+                length : length + size, tile * wide_k : (tile + 1) * wide_k
+            ]
         for ref, side in ((mine[turn], core), (partner[turn], 1 - core)):
             rows = pl.ds(pl.multiple_of((2 * there + side) * length, length), length)
-            k_all[rows, :] = ref[:, wide_k : 2 * wide_k]
+            k_all[rows, :] = ref[:length, :wide_k]
             for head in range(heads):
-                at = 2 * wide_k + head * VD
-                v_all[rows, 2 * head * VD : (2 * head + 1) * VD] = ref[:, at : at + VD]
+                at = wide_k + head * VD
+                v_all[rows, 2 * head * VD : (2 * head + 1) * VD] = ref[:length, at : at + VD]
                 v_all[rows, (2 * head + 1) * VD : (2 * head + 2) * VD] = ones
-    attend_rows(q_all, k_all, v_all, o_all, 0, core, chips, heads)
+    attend_rows(q_part, k_all, v_all, o_all, 0, core, chips, heads)
     deal(o_all, outs, chip)
 
 
-def attend_later_kernel(q_all, k_all, v_all, *refs, chips, heads, rows_from):
+def attend_later_kernel(k_all, v_all, *refs, chips, heads, rows_from):
+    queries, outs, (q_part, o_all) = refs[:chips], refs[chips : 2 * chips], refs[2 * chips :]
+    count = q_part.shape[0] // chips
     chip, core = seat()
-    attend_rows(q_all, k_all, v_all, refs[-1], rows_from, core, chips, heads)
-    deal(refs[-1], refs[:-1], chip)
-
-
-def attend(mine, partner, heads, cuts):
-    chips, (length, _), kind = len(mine), mine[0].shape, mine[0].dtype
-    whole, sizes = 2 * chips * length, [high - low for low, high in zip(cuts, cuts[1:])]
-    each = [pltpu.VMEM((size, heads * VD), kind) for size in sizes]
-    *first, q_all, k_all, v_all = pl.pallas_call(
+    for turn in range(chips):
+        q_part[pl.ds(pl.multiple_of((chip ^ turn) * count, count), count), :] = queries[turn][...]
+    attend_rows(q_part, k_all, v_all, o_all, rows_from, core, chips, heads)
+    deal(o_all, outs, chip)
+
+
+def attend(mine, partner, later, heads, cuts):
+    chips, length, kind = len(mine), cuts[-1], mine[0].dtype
+    whole, (first, second) = 2 * chips * length, (cuts[1], cuts[2] - cuts[1])
+
+    def scratch(size):
+        return [pltpu.VMEM((chips * size, heads * KD), kind), pltpu.VMEM((chips * size, heads * VD), kind)]
+
+    *one, k_all, v_all = pl.pallas_call(
         functools.partial(attend_first_kernel, chips=chips, heads=heads),
         out_shape=(
-            *(each[0],) * chips,
-            pltpu.VMEM((whole // 2, heads * KD), kind),
+            *(pltpu.VMEM((first, heads * VD), kind),) * chips,
             pltpu.VMEM((whole, heads * KD), kind),
             pltpu.VMEM((whole, 2 * heads * VD), kind),
         ),
-        scratch_shapes=[pltpu.VMEM((chips * sizes[0], heads * VD), kind)],
+        scratch_shapes=scratch(first),
         compiler_params=room(20),
         name="attend0",
     )(*in_vmem(*mine, *partner))
-    results = [first]
-    for part in range(1, len(sizes)):
-        results.append(
-            pl.pallas_call(
-                functools.partial(attend_later_kernel, chips=chips, heads=heads, rows_from=cuts[part]),
-                out_shape=(each[part],) * chips,
-                scratch_shapes=[pltpu.VMEM((chips * sizes[part], heads * VD), kind)],
-                compiler_params=room(16),
-            )(*in_vmem(q_all, k_all, v_all))
-        )
-    return results
+    other = pl.pallas_call(
+        functools.partial(attend_later_kernel, chips=chips, heads=heads, rows_from=first),
+        out_shape=(pltpu.VMEM((second, heads * VD), kind),) * chips,
+        scratch_shapes=scratch(second),
+        compiler_params=room(16),
+        name="attend1",
+    )(*in_vmem(k_all, v_all, *later))
+    return [one, other]
 
 
 def block_at(slot):
@@ -233,24 +255,34 @@
     )(*in_vmem(one, other))
 
 
-def finish_kernel(own, third, *refs):
-    lates, lasts, out = refs[: len(refs) // 2], refs[len(refs) // 2 : -1], refs[-1]
-    low = 0
-    for late, last in zip(lates, lasts):
-        rows = slice(low, low + late.shape[0])
-        total = own[rows, :] + third[rows, :].astype(jnp.float32)
-        total = total + late[...].astype(jnp.float32) + last[...].astype(jnp.float32)
-        out[rows, :] = total.astype(out.dtype)
-        low += late.shape[0]
-
-
-def finish(own, third, lates, lasts):
-    return pl.pallas_call(
-        finish_kernel,
+def finish_kernel(own, third, *refs, cuts, arrivals):
+    out, rows, sent = refs[-3:]
+    copies, at = [], 0
+    for low, high, count in zip(cuts, cuts[1:], arrivals):
+        total = own[low:high, :] + third[low:high, :].astype(jnp.float32)
+        for part in refs[at : at + count]:
+            total = total + part[...].astype(jnp.float32)
+        at += count
+        rows[low:high, :] = total.astype(rows.dtype)
+        copies.append(
+            pltpu.make_async_copy(rows.at[low:high, :], out.at[low:high, :], sent.at[len(copies)])
+        )
+        copies[-1].start()
+    for copy in copies:
+        copy.wait()
+
+
+def finish(own, third, parts, cuts):
+    flat = [part for some in parts for part in some]
+    return pl.pallas_call(
+        functools.partial(finish_kernel, cuts=cuts, arrivals=tuple(len(some) for some in parts)),
         out_shape=jax.ShapeDtypeStruct(own.shape, third.dtype),
+        in_specs=[pl.BlockSpec(memory_space=pltpu.VMEM)] * (2 + len(flat)),
+        out_specs=pl.BlockSpec(memory_space=pltpu.HBM),
+        scratch_shapes=[pltpu.VMEM(own.shape, third.dtype), pltpu.SemaphoreType.DMA((len(parts),))],
         compiler_params=room(8),
         name="finish",
-    )(*in_vmem(own, third, *lates, *lasts))
+    )(*in_vmem(own, third, *flat))
 
 
 def exchanged(queries, key_vectors, value_vectors, out_weight):
@@ -262,10 +294,12 @@
     cuts = (0, length // 2, length)
     bf16, f32 = jnp.bfloat16, jnp.float32
 
-    packed = pack(queries, key_vectors, value_vectors, chips)
+    packed = pack(queries, key_vectors, value_vectors, chips, cuts[1])
+    packed, later = packed[:chips], packed[chips:]
     mine = [packed[0]] + [swap(packed[turn], "seq", 2 * turn) for turn in range(1, chips)]
     partner = [swap(piece, "seq", 1) for piece in mine]
-    results = attend(mine, partner, heads, cuts)
+    later = [later[0]] + [swap(later[turn], "seq", 2 * turn) for turn in range(1, chips)]
+    results = attend(mine, partner, later, heads, cuts)
     weight = stage(out_weight)
     chunks = [[outs[0]] + [swap(outs[turn], "seq", 2 * turn) for turn in range(1, chips)] for outs in results]
 
@@ -273,21 +307,21 @@
         pairs = [(source, target), (ranks - 1 - source, ranks - 1 - target)]
         return lax.ppermute(value, "head", pairs)
 
-    parts = range(len(chunks))
     to_first, to_second = [None, None], [None, None]
     (to_first[0],) = project(chunks[:1], weight, columns, ((0, (0,)),), (bf16,))
     (to_second[0],) = project(chunks[:1], weight, columns, ((1, (0,)),), (bf16,))
     (to_first[1],) = project(chunks[1:], weight, columns, ((0, (0,)),), (bf16,))
-    to_second[1], to_third, own = project(
-        chunks, weight, columns, ((1, (1,)), (2, (0, 1)), (3, (0, 1))), (bf16, bf16, f32)
+    beside, to_second[1], to_third, own = project(
+        chunks, weight, columns, ((2, (1,)), (1, (1,)), (2, (0, 1)), (3, (0, 1))), (bf16, bf16, bf16, f32)
     )
-    first = [hop(to_first[part], 0, 1) for part in parts]
-    second = [hop(to_second[part], 0, 1) for part in parts]
+    first = [hop(value, 0, 1) for value in to_first]
+    second = [hop(value, 0, 1) for value in to_second]
     third = hop(to_third, 0, 1)
-    middle = [hop(join(to_first[part], first[part], 0), 1, 2) for part in parts]
-    late = [hop(join(to_second[part], second[part], 0), 1, 2) for part in parts]
-    last = [hop(join(to_third, middle[part], cuts[part]), 2, 3) for part in parts]
-    return finish(own, third, late, last)
+    joined = [join(mine, other, 0) for mine, other in zip(to_first, first)]
+    late = [hop(join(mine, other, 0), 1, 2) for mine, other in zip(to_second, second)]
+    last = hop(join(to_third, hop(joined[0], 1, 2), 0), 2, 3)
+    straight, beside = hop(joined[1], 1, 3), hop(beside, 2, 3)
+    return finish(own, third, ((late[0], last), (late[1], beside, straight)), cuts)
 
 
 def gathered(queries, key_vectors, value_vectors, out_weight):

time: 77.8 us -> 83.2 us (1.069)
  starting transfers between devices: 26.2 us -> 36.7 us
  waiting for transfers between devices: 37.8 us -> 32.4 us
    ppermute x11, starting transfers between devices: 14 us -> 21 us  [hop(): return lax.ppermute(value, 'head', pairs)]
    ppermute x11, waiting for transfers between devices: 24.5 us -> 18.6 us  [hop(): return lax.ppermute(value, 'head', pairs)]
    ppermute x13 -> x16, starting transfers between devices: 12.2 us -> 15.7 us  [swap(): return lax.ppermute(value, axis, [(i, i ^ bits) for i in range(count)])]
    ppermute x13 -> x16, waiting for transfers between devices: 13.2 us -> 13.7 us  [swap(): return lax.ppermute(value, axis, [(i, i ^ bits) for i in range(count)])]
  transfers between devices with their start and end apart: 24 -> 27, of which waited for: 10 -> 10; matrix products, arithmetic and copies ran while one was open for 0% -> 0% of each run, Pallas kernels for 11% -> 11%
where the time goes in v1:
time: 83.2 us; the launch traced here: 82.8 us
  starting transfers between devices  36.7 us (44%)
  waiting for transfers between devices  32.4 us (39%)
  Pallas kernels  13.5 us (16%)
    ppermute x11, starting transfers between devices, hop(): return lax.ppermute(value, 'head', pairs)  21 us
    ppermute x11, waiting for transfers between devices, hop(): return lax.ppermute(value, 'head', pairs)  18.6 us
    ppermute x16, starting transfers between devices, swap(): return lax.ppermute(value, axis, [(i, i ^ bits) for i in range(count)])  15.7 us
    ppermute x16, waiting for transfers between devices, swap(): return lax.ppermute(value, axis, [(i, i ^ bits) for i in range(count)])  13.7 us
    pallas_call x1, Pallas kernels, stage(): pl.pallas_call(stage_kernel, out_shape=pltpu.VMEM(weight.shape, weight.dt...  3.39 us
    pallas_call x4, Pallas kernels, project(): pl.pallas_call(functools.partial(project_kernel, chips=len(chunks[0]), ch...  3.19 us
    pallas_call x1, Pallas kernels, attend(): pl.pallas_call(functools.partial(attend_first_kernel, chips=chips, heads=...  2.18 us
    pallas_call x1, Pallas kernels, attend(): pl.pallas_call(functools.partial(attend_later_kernel, chips=chips, heads=...  1.89 us
  transfers between devices with their start and end apart: 27, of which 10 were waited for; matrix products, arithmetic and copies ran while one was open for 0% of the time, Pallas kernels for 11%

profile of v1, /device:TPU:0, one launch (start us, length us, event | category | flops | bytes accessed | tf_op | source)
XLA Modules:
  0.0 82.8 jit_solution(16630794036569946762)
XLA Ops:
  0.0 1.5 %pack.1 = (bf16[304,384]{1,0:T(8,128)(2,1)S(1)}, bf16[304,384]{1,0:T(8,128)(2,1)S(1)}, bf16[304,384]{1,0:T(8,128)(2,1)S(1)}, bf16[304,384]{1,0:T(8,128)(2,1)S(1)...) custom-call(bf16[256,512]{1,0:T(8,128)(2,1)} %q_ref.1, ...), custom_call_target="tpu_custom_call" | custom-call | tf_op jit(solution)/shard_map/pack/pallas_call | solution.py:74
  1.5 3.0 %collective-permute-start = (bf16[304,384]{1,0:T(8,128)(2,1)S(1)}, bf16[304,384]{1,0:T(8,128)(2,1)S(1)}, u32[]{:S(2)}, u32[]{:S(2)}) collective-permute-start(bf16[304,384]{1,0:T(8,128)(2,1)S(1)} %get-tuple-element.28), channel_id=1, source_target_pairs={{0,8},{4,12},{8,0},{12,4},{16,24},{20,28},{24,16},{28,20},{1,9},{5... | collective-permute-start | bytes 700424 | tf_op jit(solution)/shard_map/ppermute | solution.py:17
  4.6 1.5 %collective-permute-start.1 = (bf16[304,384]{1,0:T(8,128)(2,1)S(1)}, bf16[304,384]{1,0:T(8,128)(2,1)S(1)}, u32[]{:S(2)}, u32[]{:S(2)}) collective-permute-start(bf16[304,384]{1,0:T(8,128)(2,1)S(1)} %get-tuple-element.29), channel_id=1, source_target_pairs={{0,16},{4,20},{8,24},{12,28},{16,0},{20,4},{24,8},{28,12},{1,17},{... | collective-permute-start | bytes 700424 | tf_op jit(solution)/shard_map/ppermute | solution.py:17
  6.1 0.0 collective-permute-start.2
  6.1 0.0 collective-permute-start.3
  6.1 5.0 %collective-permute-done.refs_1_ = bf16[304,384]{1,0:T(8,128)(2,1)S(1)} collective-permute-done((bf16[304,384]{1,0:T(8,128)(2,1)S(1)}, bf16[304,384]{1,0:T(8,128)(2,1)S(1)}, u32[]{:S(2)}, u32[]{:S(2)}) %collective-permute-start) | collective-permute-done | bytes 233504 | tf_op jit(solution)/shard_map/ppermute | solution.py:17
  11.1 0.0 collective-permute-start.4
  11.1 5.6 %collective-permute-done.1.refs_2_ = bf16[304,384]{1,0:T(8,128)(2,1)S(1)} collective-permute-done((bf16[304,384]{1,0:T(8,128)(2,1)S(1)}, bf16[304,384]{1,0:T(8,128)(2,1)S(1)}, u32[]{:S(2)}, u32[]{:S(2)}) %collective-permute-start.1) | collective-permute-done | bytes 233504 | tf_op jit(solution)/shard_map/ppermute | solution.py:17
  16.7 0.0 collective-permute-start.5
  16.7 0.0 collective-permute-done.2.refs_3_
  16.7 0.5 collective-permute-start.6
  17.2 0.0 collective-permute-done.3.refs_4_
  17.2 0.0 collective-permute-done.4.refs_5_
  17.2 1.0 %collective-permute-done.5.refs_6_ = bf16[304,384]{1,0:T(8,128)(2,1)S(1)} collective-permute-done((bf16[304,384]{1,0:T(8,128)(2,1)S(1)}, bf16[304,384]{1,0:T(8,128)(2,1)S(1)}, u32[]{:S(2)}, u32[]{:S(2)}) %collective-permute-start.5) | collective-permute-done | bytes 233504 | tf_op jit(solution)/shard_map/ppermute | solution.py:17
  18.2 0.3 collective-permute-done.6.refs_7_
  18.6 2.2 %attend0.1 = (bf16[128,256]{1,0:T(8,128)(2,1)S(1)}, bf16[128,256]{1,0:T(8,128)(2,1)S(1)}, bf16[128,256]{1,0:T(8,128)(2,1)S(1)}, bf16[128,256]{1,0:T(8,128)(2,1)S...) custom-call(bf16[304,384]{1,0:T(8,128)(2,1)S(1)} %get-tuple-element.27.refs_0_, ...), custom_call_target="tpu_custom_call" | custom-call | tf_op jit(solution)/shard_map/attend0/pallas_call | solution.py:183
  20.7 1.0 %collective-permute-start.7 = (bf16[128,256]{1,0:T(8,128)(2,1)S(1)}, bf16[128,256]{1,0:T(8,128)(2,1)S(1)}, u32[]{:S(2)}, u32[]{:S(2)}) collective-permute-start(bf16[128,256]{1,0:T(8,128)(2,1)S(1)} %get-tuple-element.32), channel_id=1, source_target_pairs={{0,8},{4,12},{8,0},{12,4},{16,24},{20,28},{24,16},{28,20},{1,9},{5... | collective-permute-start | bytes 196616 | tf_op jit(solution)/shard_map/ppermute | solution.py:17
  21.7 1.1 %collective-permute-start.10 = (bf16[128,128]{1,0:T(8,128)(2,1)S(1)}, bf16[128,128]{1,0:T(8,128)(2,1)S(1)}, u32[]{:S(2)}, u32[]{:S(2)}) collective-permute-start(bf16[128,128]{1,0:T(8,128)(2,1)S(1)} %get-tuple-element.38), channel_id=1, source_target_pairs={{0,8},{4,12},{8,0},{12,4},{16,24},{20,28},{24,16},{28,20},{1,9},{5... | collective-permute-start | bytes 98312 | tf_op jit(solution)/shard_map/ppermute | solution.py:17
  22.8 1.5 %collective-permute-start.11 = (bf16[128,128]{1,0:T(8,128)(2,1)S(1)}, bf16[128,128]{1,0:T(8,128)(2,1)S(1)}, u32[]{:S(2)}, u32[]{:S(2)}) collective-permute-start(bf16[128,128]{1,0:T(8,128)(2,1)S(1)} %get-tuple-element.39), channel_id=1, source_target_pairs={{0,16},{4,20},{8,24},{12,28},{16,0},{20,4},{24,8},{28,12},{1,17},{... | collective-permute-start | bytes 98312 | tf_op jit(solution)/shard_map/ppermute | solution.py:17
  24.4 0.8 %collective-permute-start.12 = (bf16[128,128]{1,0:T(8,128)(2,1)S(1)}, bf16[128,128]{1,0:T(8,128)(2,1)S(1)}, u32[]{:S(2)}, u32[]{:S(2)}) collective-permute-start(bf16[128,128]{1,0:T(8,128)(2,1)S(1)} %get-tuple-element.40), channel_id=1, source_target_pairs={{0,24},{4,28},{8,16},{12,20},{16,8},{20,12},{24,0},{28,4},{1,25},{... | collective-permute-start | bytes 98312 | tf_op jit(solution)/shard_map/ppermute | solution.py:17
  25.2 1.2 %collective-permute-start.8 = (bf16[128,256]{1,0:T(8,128)(2,1)S(1)}, bf16[128,256]{1,0:T(8,128)(2,1)S(1)}, u32[]{:S(2)}, u32[]{:S(2)}) collective-permute-start(bf16[128,256]{1,0:T(8,128)(2,1)S(1)} %get-tuple-element.33), channel_id=1, source_target_pairs={{0,16},{4,20},{8,24},{12,28},{16,0},{20,4},{24,8},{28,12},{1,17},{... | collective-permute-start | bytes 196616 | tf_op jit(solution)/shard_map/ppermute | solution.py:17
  26.4 0.0 collective-permute-done.10.refs_1_
  26.4 1.4 %collective-permute-start.9 = (bf16[128,256]{1,0:T(8,128)(2,1)S(1)}, bf16[128,256]{1,0:T(8,128)(2,1)S(1)}, u32[]{:S(2)}, u32[]{:S(2)}) collective-permute-start(bf16[128,256]{1,0:T(8,128)(2,1)S(1)} %get-tuple-element.34), channel_id=1, source_target_pairs={{0,24},{4,28},{8,16},{12,20},{16,8},{20,12},{24,0},{28,4},{1,25},{... | collective-permute-start | bytes 196616 | tf_op jit(solution)/shard_map/ppermute | solution.py:17
  27.8 0.0 collective-permute-done.11.refs_2_
  27.8 1.8 %collective-permute-done.12.refs_3_ = bf16[128,128]{1,0:T(8,128)(2,1)S(1)} collective-permute-done((bf16[128,128]{1,0:T(8,128)(2,1)S(1)}, bf16[128,128]{1,0:T(8,128)(2,1)S(1)}, u32[]{:S(2)}, u32[]{:S(2)}) %collective-permute-start.12) | collective-permute-done | bytes 32800 | tf_op jit(solution)/shard_map/ppermute | solution.py:17
  29.6 1.9 %attend1.1 = (bf16[128,256]{1,0:T(8,128)(2,1)S(1)}, bf16[128,256]{1,0:T(8,128)(2,1)S(1)}, bf16[128,256]{1,0:T(8,128)(2,1)S(1)}, bf16[128,256]{1,0:T(8,128)(2,1)S(1)}) custom-call(bf16[2048,128]{1,0:T(8,128)(2,1)S(1)} %get-tuple-element.35.k_all, bf16[2048,512]{1,0:T(8,128)(2,1)S(1)} %get-tuple-element.36.v_all, ...), custom_call_target="tpu_custom_call" | custom-call | tf_op jit(solution)/shard_map/attend1/pallas_call | solution.py:194
  31.5 0.2 collective-permute-start.13
  31.7 0.9 %collective-permute-start.14 = (bf16[128,256]{1,0:T(8,128)(2,1)S(1)}, bf16[128,256]{1,0:T(8,128)(2,1)S(1)}, u32[]{:S(2)}, u32[]{:S(2)}) collective-permute-start(bf16[128,256]{1,0:T(8,128)(2,1)S(1)} %get-tuple-element.43), channel_id=1, source_target_pairs={{0,16},{4,20},{8,24},{12,28},{16,0},{20,4},{24,8},{28,12},{1,17},{... | collective-permute-start | bytes 196616 | tf_op jit(solution)/shard_map/ppermute | solution.py:17
  32.6 0.0 collective-permute-done.7.refs_1_
  32.6 2.5 %collective-permute-start.15 = (bf16[128,256]{1,0:T(8,128)(2,1)S(1)}, bf16[128,256]{1,0:T(8,128)(2,1)S(1)}, u32[]{:S(2)}, u32[]{:S(2)}) collective-permute-start(bf16[128,256]{1,0:T(8,128)(2,1)S(1)} %get-tuple-element.44), channel_id=1, source_target_pairs={{0,24},{4,28},{8,16},{12,20},{16,8},{20,12},{24,0},{28,4},{1,25},{... | collective-permute-start | bytes 196616 | tf_op jit(solution)/shard_map/ppermute | solution.py:17
  35.1 3.4 %stage.1.refs_8_.refs_4_ = bf16[1024,4096]{1,0:T(8,128)(2,1)S(1)} custom-call(bf16[1024,4096]{1,0:T(8,128)(2,1)} %w_ref.1), custom_call_target="tpu_custom_call" | custom-call | tf_op jit(solution)/shard_map/stage/pallas_call | solution.py:94
  38.5 0.0 collective-permute-done.8.refs_2_
  38.5 0.0 collective-permute-done.9.refs_3_
  38.5 0.5 shard_map.48.one
  38.9 3.5 %collective-permute-start.19 = (bf16[128,1024]{1,0:T(8,128)(2,1)S(1)}, bf16[128,1024]{1,0:T(8,128)(2,1)S(1)}, u32[]{:S(2)}, u32[]{:S(2)}) collective-permute-start(bf16[128,1024]{1,0:T(8,128)(2,1)S(1)} %shard_map.48.one), channel_id=1, source_target_pairs={{0,1},{3,2},{4,5},{7,6},{8,9},{11,10},{12,13},{15,14},{16,17},{19,... | collective-permute-start | bytes 786440 | tf_op jit(solution)/shard_map/ppermute | solution.py:308
  42.4 0.0 collective-permute-done.13.refs_5_.refs_1_
  42.5 0.0 collective-permute-done.15.refs_7_.refs_3_
  42.5 1.8 %shard_map.46 = (bf16[128,1024]{1,0:T(8,128)(2,1)S(1)}, bf16[128,1024]{1,0:T(8,128)(2,1)S(1)}, bf16[256,1024]{1,0:T(8,128)(2,1)S(1)}, f32[256,1024]{1,0:T(8,128)S(1)}) custom-call(bf16[128,256]{1,0:T(8,128)(2,1)S(1)} %get-tuple-element.31.refs_0_, bf16[128,256]{1,0:T(8,128)(2,1)S(1)} %collective-permute-done.7.refs_1_, ...), custom_call_target="tpu_custom_call" | custom-call | tf_op jit(solution)/shard_map/pallas_call | solution.py:234
  44.3 1.3 %collective-permute-start.22 = (bf16[128,1024]{1,0:T(8,128)(2,1)S(1)}, bf16[128,1024]{1,0:T(8,128)(2,1)S(1)}, u32[]{:S(2)}, u32[]{:S(2)}) collective-permute-start(bf16[128,1024]{1,0:T(8,128)(2,1)S(1)} %get-tuple-element.47.one), channel_id=1, source_target_pairs={{0,1},{3,2},{4,5},{7,6},{8,9},{11,10},{12,13},{15,14},{16,17},{19,... | collective-permute-start | bytes 786440 | tf_op jit(solution)/shard_map/ppermute | solution.py:308
  45.6 0.5 shard_map.47.one
  46.1 1.3 %collective-permute-start.17 = (bf16[128,1024]{1,0:T(8,128)(2,1)S(1)}, bf16[128,1024]{1,0:T(8,128)(2,1)S(1)}, u32[]{:S(2)}, u32[]{:S(2)}) collective-permute-start(bf16[128,1024]{1,0:T(8,128)(2,1)S(1)} %shard_map.47.one), channel_id=1, source_target_pairs={{0,1},{3,2},{4,5},{7,6},{8,9},{11,10},{12,13},{15,14},{16,17},{19,... | collective-permute-start | bytes 786440 | tf_op jit(solution)/shard_map/ppermute | solution.py:308
  47.4 1.3 %collective-permute-start.24 = (bf16[128,1024]{1,0:T(8,128)(2,1)S(1)}, bf16[128,1024]{1,0:T(8,128)(2,1)S(1)}, u32[]{:S(2)}, u32[]{:S(2)}) collective-permute-start(bf16[128,1024]{1,0:T(8,128)(2,1)S(1)} %get-tuple-element.48), channel_id=1, source_target_pairs={{2,3},{1,0},{6,7},{5,4},{10,11},{9,8},{14,15},{13,12},{18,19},{17,... | collective-permute-start | bytes 786440 | tf_op jit(solution)/shard_map/ppermute | solution.py:308
  48.7 0.5 shard_map.49.one
  49.2 4.6 %collective-permute-start.25 = (bf16[128,1024]{1,0:T(8,128)(2,1)S(1)}, bf16[128,1024]{1,0:T(8,128)(2,1)S(1)}, u32[]{:S(2)}, u32[]{:S(2)}) collective-permute-start(bf16[128,1024]{1,0:T(8,128)(2,1)S(1)} %shard_map.49.one), channel_id=1, source_target_pairs={{0,1},{3,2},{4,5},{7,6},{8,9},{11,10},{12,13},{15,14},{16,17},{19,... | collective-permute-start | bytes 786440 | tf_op jit(solution)/shard_map/ppermute | solution.py:308
  53.8 0.1 join.6
  53.8 0.7 collective-permute-start.20
  54.5 0.2 collective-permute-done.22.other
  54.7 4.4 %collective-permute-start.16 = (bf16[256,1024]{1,0:T(8,128)(2,1)S(1)}, bf16[256,1024]{1,0:T(8,128)(2,1)S(1)}, u32[]{:S(2)}, u32[]{:S(2)}) collective-permute-start(bf16[256,1024]{1,0:T(8,128)(2,1)S(1)} %get-tuple-element.46.one), channel_id=1, source_target_pairs={{0,1},{3,2},{4,5},{7,6},{8,9},{11,10},{12,13},{15,14},{16,17},{19,... | collective-permute-start | bytes 1572872 | tf_op jit(solution)/shard_map/ppermute | solution.py:308
  59.1 0.1 join.8
  59.2 1.1 %collective-permute-done.17.other = bf16[128,1024]{1,0:T(8,128)(2,1)S(1)} collective-permute-done((bf16[128,1024]{1,0:T(8,128)(2,1)S(1)}, bf16[128,1024]{1,0:T(8,128)(2,1)S(1)}, u32[]{:S(2)}, u32[]{:S(2)}) %collective-permute-start.17) | collective-permute-done | bytes 262176 | tf_op jit(solution)/shard_map/ppermute | solution.py:308
  60.3 0.7 collective-permute-start.23
  61.0 0.1 join.5
  61.1 4.9 %collective-permute-done.25.other = bf16[128,1024]{1,0:T(8,128)(2,1)S(1)} collective-permute-done((bf16[128,1024]{1,0:T(8,128)(2,1)S(1)}, bf16[128,1024]{1,0:T(8,128)(2,1)S(1)}, u32[]{:S(2)}, u32[]{:S(2)}) %collective-permute-start.25) | collective-permute-done | bytes 262176 | tf_op jit(solution)/shard_map/ppermute | solution.py:308
  66.0 0.7 collective-permute-start.18
  66.6 0.1 join.9
  66.7 1.3 %collective-permute-start.26 = (bf16[128,1024]{1,0:T(8,128)(2,1)S(1)}, bf16[128,1024]{1,0:T(8,128)(2,1)S(1)}, u32[]{:S(2)}, u32[]{:S(2)}) collective-permute-start(bf16[128,1024]{1,0:T(8,128)(2,1)S(1)} %join.9), channel_id=1, source_target_pairs={{1,3},{2,0},{5,7},{6,4},{9,11},{10,8},{13,15},{14,12},{17,19},{18,... | collective-permute-start | bytes 786440 | tf_op jit(solution)/shard_map/ppermute | solution.py:308
  68.0 0.1 join.7
  68.1 0.0 collective-permute-done.24.refs_3_
  68.1 1.3 %collective-permute-start.21 = (bf16[128,1024]{1,0:T(8,128)(2,1)S(1)}, bf16[128,1024]{1,0:T(8,128)(2,1)S(1)}, u32[]{:S(2)}, u32[]{:S(2)}) collective-permute-start(bf16[128,1024]{1,0:T(8,128)(2,1)S(1)} %join.7), channel_id=1, source_target_pairs={{2,3},{1,0},{6,7},{5,4},{10,11},{9,8},{14,15},{13,12},{18,19},{17,... | collective-permute-start | bytes 786440 | tf_op jit(solution)/shard_map/ppermute | solution.py:308
  69.4 0.0 collective-permute-done.18.refs_0_
  69.4 10.0 %collective-permute-done.26.refs_4_ = bf16[128,1024]{1,0:T(8,128)(2,1)S(1)} collective-permute-done((bf16[128,1024]{1,0:T(8,128)(2,1)S(1)}, bf16[128,1024]{1,0:T(8,128)(2,1)S(1)}, u32[]{:S(2)}, u32[]{:S(2)}) %collective-permute-start.26) | collective-permute-done | bytes 262176 | tf_op jit(solution)/shard_map/ppermute | solution.py:308
  79.4 0.0 collective-permute-done.16.third
  79.5 2.4 %collective-permute-done.21.refs_1_ = bf16[128,1024]{1,0:T(8,128)(2,1)S(1)} collective-permute-done((bf16[128,1024]{1,0:T(8,128)(2,1)S(1)}, bf16[128,1024]{1,0:T(8,128)(2,1)S(1)}, u32[]{:S(2)}, u32[]{:S(2)}) %collective-permute-start.21) | collective-permute-done | bytes 262176 | tf_op jit(solution)/shard_map/ppermute | solution.py:308
  81.8 1.0 %finish.1 = bf16[256,1024]{1,0:T(8,128)(2,1)} custom-call(f32[256,1024]{1,0:T(8,128)S(1)} %get-tuple-element.45.own, bf16[256,1024]{1,0:T(8,128)(2,1)S(1)} %collective-permute-done.16.third, bf16[128,1024]{1,0:T(8,128)(2,1)S(1)} %collective-permute-done.18.refs_0_, bf16[128,1024]{1,0:T(8,128)(2,1)S(1)} %collective-permute-done.21.refs_1_, ...), custom_call_target="tpu_custom_call" | custom-call | tf_op jit(solution)/shard_map/finish/pallas_call | solution.py:277
  (4 shorter events, 0.0 us)
Async XLA Ops:
  1.5 9.6 %collective-permute-start = (bf16[304,384]{1,0:T(8,128)(2,1)S(1)}, bf16[304,384]{1,0:T(8,128)(2,1)S(1)}, u32[]{:S(2)}, u32[]{:S(2)}) collective-permute-start(bf16[304,384]{1,0:T(8,128)(2,1)S(1)} %get-tuple-element.28), channel_id=1, source_target_pairs={{0,8},{4,12},{8,0},{12,4},{16,24},{20,28},{24,16},{28,20},{1,9},{5... | collective-permute-start | bytes 700424 | tf_op jit(solution)/shard_map/ppermute | solution.py:17
  4.6 12.2 %collective-permute-start.1 = (bf16[304,384]{1,0:T(8,128)(2,1)S(1)}, bf16[304,384]{1,0:T(8,128)(2,1)S(1)}, u32[]{:S(2)}, u32[]{:S(2)}) collective-permute-start(bf16[304,384]{1,0:T(8,128)(2,1)S(1)} %get-tuple-element.29), channel_id=1, source_target_pairs={{0,16},{4,20},{8,24},{12,28},{16,0},{20,4},{24,8},{28,12},{1,17},{... | collective-permute-start | bytes 700424 | tf_op jit(solution)/shard_map/ppermute | solution.py:17
  6.1 10.6 %collective-permute-start.2 = (bf16[304,384]{1,0:T(8,128)(2,1)S(1)}, bf16[304,384]{1,0:T(8,128)(2,1)S(1)}, u32[]{:S(2)}, u32[]{:S(2)}) collective-permute-start(bf16[304,384]{1,0:T(8,128)(2,1)S(1)} %get-tuple-element.30), channel_id=1, source_target_pairs={{0,24},{4,28},{8,16},{12,20},{16,8},{20,12},{24,0},{28,4},{1,25},{... | collective-permute-start | bytes 700424 | tf_op jit(solution)/shard_map/ppermute | solution.py:17
  6.1 11.1 %collective-permute-start.3 = (bf16[304,384]{1,0:T(8,128)(2,1)S(1)}, bf16[304,384]{1,0:T(8,128)(2,1)S(1)}, u32[]{:S(2)}, u32[]{:S(2)}) collective-permute-start(bf16[304,384]{1,0:T(8,128)(2,1)S(1)} %get-tuple-element.27.refs_0_), channel_id=1, source_target_pairs={{0,4},{4,0},{8,12},{12,8},{16,20},{20,16},{24,28},{28,24},{1,5},{5... | collective-permute-start | bytes 700424 | tf_op jit(solution)/shard_map/ppermute | solution.py:17
  11.1 6.1 %collective-permute-start.4 = (bf16[304,384]{1,0:T(8,128)(2,1)S(1)}, bf16[304,384]{1,0:T(8,128)(2,1)S(1)}, u32[]{:S(2)}, u32[]{:S(2)}) collective-permute-start(bf16[304,384]{1,0:T(8,128)(2,1)S(1)} %collective-permute-done.refs_1_), channel_id=1, source_target_pairs={{0,4},{4,0},{8,12},{12,8},{16,20},{20,16},{24,28},{28,24},{1,5},{5... | collective-permute-start | bytes 700424 | tf_op jit(solution)/shard_map/ppermute | solution.py:17
  16.7 1.5 %collective-permute-start.5 = (bf16[304,384]{1,0:T(8,128)(2,1)S(1)}, bf16[304,384]{1,0:T(8,128)(2,1)S(1)}, u32[]{:S(2)}, u32[]{:S(2)}) collective-permute-start(bf16[304,384]{1,0:T(8,128)(2,1)S(1)} %collective-permute-done.1.refs_2_), channel_id=1, source_target_pairs={{0,4},{4,0},{8,12},{12,8},{16,20},{20,16},{24,28},{28,24},{1,5},{5... | collective-permute-start | bytes 700424 | tf_op jit(solution)/shard_map/ppermute | solution.py:17
  16.7 1.8 %collective-permute-start.6 = (bf16[304,384]{1,0:T(8,128)(2,1)S(1)}, bf16[304,384]{1,0:T(8,128)(2,1)S(1)}, u32[]{:S(2)}, u32[]{:S(2)}) collective-permute-start(bf16[304,384]{1,0:T(8,128)(2,1)S(1)} %collective-permute-done.2.refs_3_), channel_id=1, source_target_pairs={{0,4},{4,0},{8,12},{12,8},{16,20},{20,16},{24,28},{28,24},{1,5},{5... | collective-permute-start | bytes 700424 | tf_op jit(solution)/shard_map/ppermute | solution.py:17
  20.7 11.8 %collective-permute-start.7 = (bf16[128,256]{1,0:T(8,128)(2,1)S(1)}, bf16[128,256]{1,0:T(8,128)(2,1)S(1)}, u32[]{:S(2)}, u32[]{:S(2)}) collective-permute-start(bf16[128,256]{1,0:T(8,128)(2,1)S(1)} %get-tuple-element.32), channel_id=1, source_target_pairs={{0,8},{4,12},{8,0},{12,4},{16,24},{20,28},{24,16},{28,20},{1,9},{5... | collective-permute-start | bytes 196616 | tf_op jit(solution)/shard_map/ppermute | solution.py:17
  21.7 4.7 %collective-permute-start.10 = (bf16[128,128]{1,0:T(8,128)(2,1)S(1)}, bf16[128,128]{1,0:T(8,128)(2,1)S(1)}, u32[]{:S(2)}, u32[]{:S(2)}) collective-permute-start(bf16[128,128]{1,0:T(8,128)(2,1)S(1)} %get-tuple-element.38), channel_id=1, source_target_pairs={{0,8},{4,12},{8,0},{12,4},{16,24},{20,28},{24,16},{28,20},{1,9},{5... | collective-permute-start | bytes 98312 | tf_op jit(solution)/shard_map/ppermute | solution.py:17
  22.8 5.0 %collective-permute-start.11 = (bf16[128,128]{1,0:T(8,128)(2,1)S(1)}, bf16[128,128]{1,0:T(8,128)(2,1)S(1)}, u32[]{:S(2)}, u32[]{:S(2)}) collective-permute-start(bf16[128,128]{1,0:T(8,128)(2,1)S(1)} %get-tuple-element.39), channel_id=1, source_target_pairs={{0,16},{4,20},{8,24},{12,28},{16,0},{20,4},{24,8},{28,12},{1,17},{... | collective-permute-start | bytes 98312 | tf_op jit(solution)/shard_map/ppermute | solution.py:17
  24.4 5.2 %collective-permute-start.12 = (bf16[128,128]{1,0:T(8,128)(2,1)S(1)}, bf16[128,128]{1,0:T(8,128)(2,1)S(1)}, u32[]{:S(2)}, u32[]{:S(2)}) collective-permute-start(bf16[128,128]{1,0:T(8,128)(2,1)S(1)} %get-tuple-element.40), channel_id=1, source_target_pairs={{0,24},{4,28},{8,16},{12,20},{16,8},{20,12},{24,0},{28,4},{1,25},{... | collective-permute-start | bytes 98312 | tf_op jit(solution)/shard_map/ppermute | solution.py:17
  25.2 13.3 %collective-permute-start.8 = (bf16[128,256]{1,0:T(8,128)(2,1)S(1)}, bf16[128,256]{1,0:T(8,128)(2,1)S(1)}, u32[]{:S(2)}, u32[]{:S(2)}) collective-permute-start(bf16[128,256]{1,0:T(8,128)(2,1)S(1)} %get-tuple-element.33), channel_id=1, source_target_pairs={{0,16},{4,20},{8,24},{12,28},{16,0},{20,4},{24,8},{28,12},{1,17},{... | collective-permute-start | bytes 196616 | tf_op jit(solution)/shard_map/ppermute | solution.py:17
  26.4 12.1 %collective-permute-start.9 = (bf16[128,256]{1,0:T(8,128)(2,1)S(1)}, bf16[128,256]{1,0:T(8,128)(2,1)S(1)}, u32[]{:S(2)}, u32[]{:S(2)}) collective-permute-start(bf16[128,256]{1,0:T(8,128)(2,1)S(1)} %get-tuple-element.34), channel_id=1, source_target_pairs={{0,24},{4,28},{8,16},{12,20},{16,8},{20,12},{24,0},{28,4},{1,25},{... | collective-permute-start | bytes 196616 | tf_op jit(solution)/shard_map/ppermute | solution.py:17
  31.5 11.0 %collective-permute-start.13 = (bf16[128,256]{1,0:T(8,128)(2,1)S(1)}, bf16[128,256]{1,0:T(8,128)(2,1)S(1)}, u32[]{:S(2)}, u32[]{:S(2)}) collective-permute-start(bf16[128,256]{1,0:T(8,128)(2,1)S(1)} %get-tuple-element.42), channel_id=1, source_target_pairs={{0,8},{4,12},{8,0},{12,4},{16,24},{20,28},{24,16},{28,20},{1,9},{5... | collective-permute-start | bytes 196616 | tf_op jit(solution)/shard_map/ppermute | solution.py:17
  31.7 10.8 %collective-permute-start.14 = (bf16[128,256]{1,0:T(8,128)(2,1)S(1)}, bf16[128,256]{1,0:T(8,128)(2,1)S(1)}, u32[]{:S(2)}, u32[]{:S(2)}) collective-permute-start(bf16[128,256]{1,0:T(8,128)(2,1)S(1)} %get-tuple-element.43), channel_id=1, source_target_pairs={{0,16},{4,20},{8,24},{12,28},{16,0},{20,4},{24,8},{28,12},{1,17},{... | collective-permute-start | bytes 196616 | tf_op jit(solution)/shard_map/ppermute | solution.py:17
  32.6 9.9 %collective-permute-start.15 = (bf16[128,256]{1,0:T(8,128)(2,1)S(1)}, bf16[128,256]{1,0:T(8,128)(2,1)S(1)}, u32[]{:S(2)}, u32[]{:S(2)}) collective-permute-start(bf16[128,256]{1,0:T(8,128)(2,1)S(1)} %get-tuple-element.44), channel_id=1, source_target_pairs={{0,24},{4,28},{8,16},{12,20},{16,8},{20,12},{24,0},{28,4},{1,25},{... | collective-permute-start | bytes 196616 | tf_op jit(solution)/shard_map/ppermute | solution.py:17
  38.9 14.8 %collective-permute-start.19 = (bf16[128,1024]{1,0:T(8,128)(2,1)S(1)}, bf16[128,1024]{1,0:T(8,128)(2,1)S(1)}, u32[]{:S(2)}, u32[]{:S(2)}) collective-permute-start(bf16[128,1024]{1,0:T(8,128)(2,1)S(1)} %shard_map.48.one), channel_id=1, source_target_pairs={{0,1},{3,2},{4,5},{7,6},{8,9},{11,10},{12,13},{15,14},{16,17},{19,... | collective-permute-start | bytes 786440 | tf_op jit(solution)/shard_map/ppermute | solution.py:308
  44.3 10.4 %collective-permute-start.22 = (bf16[128,1024]{1,0:T(8,128)(2,1)S(1)}, bf16[128,1024]{1,0:T(8,128)(2,1)S(1)}, u32[]{:S(2)}, u32[]{:S(2)}) collective-permute-start(bf16[128,1024]{1,0:T(8,128)(2,1)S(1)} %get-tuple-element.47.one), channel_id=1, source_target_pairs={{0,1},{3,2},{4,5},{7,6},{8,9},{11,10},{12,13},{15,14},{16,17},{19,... | collective-permute-start | bytes 786440 | tf_op jit(solution)/shard_map/ppermute | solution.py:308
  46.1 14.3 %collective-permute-start.17 = (bf16[128,1024]{1,0:T(8,128)(2,1)S(1)}, bf16[128,1024]{1,0:T(8,128)(2,1)S(1)}, u32[]{:S(2)}, u32[]{:S(2)}) collective-permute-start(bf16[128,1024]{1,0:T(8,128)(2,1)S(1)} %shard_map.47.one), channel_id=1, source_target_pairs={{0,1},{3,2},{4,5},{7,6},{8,9},{11,10},{12,13},{15,14},{16,17},{19,... | collective-permute-start | bytes 786440 | tf_op jit(solution)/shard_map/ppermute | solution.py:308
  47.4 20.7 %collective-permute-start.24 = (bf16[128,1024]{1,0:T(8,128)(2,1)S(1)}, bf16[128,1024]{1,0:T(8,128)(2,1)S(1)}, u32[]{:S(2)}, u32[]{:S(2)}) collective-permute-start(bf16[128,1024]{1,0:T(8,128)(2,1)S(1)} %get-tuple-element.48), channel_id=1, source_target_pairs={{2,3},{1,0},{6,7},{5,4},{10,11},{9,8},{14,15},{13,12},{18,19},{17,... | collective-permute-start | bytes 786440 | tf_op jit(solution)/shard_map/ppermute | solution.py:308
  49.2 16.8 %collective-permute-start.25 = (bf16[128,1024]{1,0:T(8,128)(2,1)S(1)}, bf16[128,1024]{1,0:T(8,128)(2,1)S(1)}, u32[]{:S(2)}, u32[]{:S(2)}) collective-permute-start(bf16[128,1024]{1,0:T(8,128)(2,1)S(1)} %shard_map.49.one), channel_id=1, source_target_pairs={{0,1},{3,2},{4,5},{7,6},{8,9},{11,10},{12,13},{15,14},{16,17},{19,... | collective-permute-start | bytes 786440 | tf_op jit(solution)/shard_map/ppermute | solution.py:308
  53.8 12.9 %collective-permute-start.20 = (bf16[128,1024]{1,0:T(8,128)(2,1)S(1)}, bf16[128,1024]{1,0:T(8,128)(2,1)S(1)}, u32[]{:S(2)}, u32[]{:S(2)}) collective-permute-start(bf16[128,1024]{1,0:T(8,128)(2,1)S(1)} %join.6), channel_id=1, source_target_pairs={{1,2},{2,1},{5,6},{6,5},{9,10},{10,9},{13,14},{14,13},{17,18},{18,... | collective-permute-start | bytes 786440 | tf_op jit(solution)/shard_map/ppermute | solution.py:308
  54.7 24.7 %collective-permute-start.16 = (bf16[256,1024]{1,0:T(8,128)(2,1)S(1)}, bf16[256,1024]{1,0:T(8,128)(2,1)S(1)}, u32[]{:S(2)}, u32[]{:S(2)}) collective-permute-start(bf16[256,1024]{1,0:T(8,128)(2,1)S(1)} %get-tuple-element.46.one), channel_id=1, source_target_pairs={{0,1},{3,2},{4,5},{7,6},{8,9},{11,10},{12,13},{15,14},{16,17},{19,... | collective-permute-start | bytes 1572872 | tf_op jit(solution)/shard_map/ppermute | solution.py:308
  60.3 9.1 %collective-permute-start.23 = (bf16[128,1024]{1,0:T(8,128)(2,1)S(1)}, bf16[128,1024]{1,0:T(8,128)(2,1)S(1)}, u32[]{:S(2)}, u32[]{:S(2)}) collective-permute-start(bf16[128,1024]{1,0:T(8,128)(2,1)S(1)} %join.8), channel_id=1, source_target_pairs={{1,2},{2,1},{5,6},{6,5},{9,10},{10,9},{13,14},{14,13},{17,18},{18,... | collective-permute-start | bytes 786440 | tf_op jit(solution)/shard_map/ppermute | solution.py:308
  66.0 3.4 %collective-permute-start.18 = (bf16[128,1024]{1,0:T(8,128)(2,1)S(1)}, bf16[128,1024]{1,0:T(8,128)(2,1)S(1)}, u32[]{:S(2)}, u32[]{:S(2)}) collective-permute-start(bf16[128,1024]{1,0:T(8,128)(2,1)S(1)} %join.5), channel_id=1, source_target_pairs={{1,2},{2,1},{5,6},{6,5},{9,10},{10,9},{13,14},{14,13},{17,18},{18,... | collective-permute-start | bytes 786440 | tf_op jit(solution)/shard_map/ppermute | solution.py:308
  66.7 12.7 %collective-permute-start.26 = (bf16[128,1024]{1,0:T(8,128)(2,1)S(1)}, bf16[128,1024]{1,0:T(8,128)(2,1)S(1)}, u32[]{:S(2)}, u32[]{:S(2)}) collective-permute-start(bf16[128,1024]{1,0:T(8,128)(2,1)S(1)} %join.9), channel_id=1, source_target_pairs={{1,3},{2,0},{5,7},{6,4},{9,11},{10,8},{13,15},{14,12},{17,19},{18,... | collective-permute-start | bytes 786440 | tf_op jit(solution)/shard_map/ppermute | solution.py:308
  68.1 13.7 %collective-permute-start.21 = (bf16[128,1024]{1,0:T(8,128)(2,1)S(1)}, bf16[128,1024]{1,0:T(8,128)(2,1)S(1)}, u32[]{:S(2)}, u32[]{:S(2)}) collective-permute-start(bf16[128,1024]{1,0:T(8,128)(2,1)S(1)} %join.7), channel_id=1, source_target_pairs={{2,3},{1,0},{6,7},{5,4},{10,11},{9,8},{14,15},{13,12},{18,19},{17,... | collective-permute-start | bytes 786440 | tf_op jit(solution)/shard_map/ppermute | solution.py:308

commit v2 on v1

--- a/solution.py
+++ b/solution.py
@@ -104,31 +104,36 @@
 def attend_rows(q_part, k_all, v_all, o_all, rows_from, core, chips, heads):
     length, wide_k = k_all.shape[0] // (2 * chips), heads * KD
     count = o_all.shape[0] // chips
-    row = lax.broadcasted_iota(jnp.int32, (count, 2 * length), 0) + (core * length + rows_from)
-    seen = lax.broadcasted_iota(jnp.int32, (count, 2 * length), 1) <= row
+    reach = length + rows_from + count
+    row = lax.broadcasted_iota(jnp.int32, (count, reach), 0) + (core * length + rows_from)
+    seen = lax.broadcasted_iota(jnp.int32, (count, reach), 1) <= row
+    seen = jnp.concatenate([seen] * heads, axis=0)
     lane = lax.broadcasted_iota(jnp.int32, (count, wide_k), 1) // KD
     for index in range(chips):
         q = q_part[index * count : (index + 1) * count, :] * jnp.bfloat16(KD ** (-0.5))
+        stacked = jnp.concatenate([jnp.where(lane == head, q, jnp.bfloat16(0)) for head in range(heads)], axis=0)
+        total = denominator = None
+        for block in range(index + 1):
+            at = 2 * block * length
+            rows = slice(at, at + (reach if block == index else 2 * length))
+            scores = lax.dot_general(
+                stacked, k_all[rows, :], (((1,), (1,)), ((), ())), preferred_element_type=jnp.float32
+            )
+            raised = scores + 1.0
+            weights = raised * raised + 1.0
+            if block == index:
+                weights = jnp.where(seen, weights, 0.0)
+            weights = weights.astype(jnp.bfloat16)
+            part = jnp.dot(weights, v_all[rows, :], preferred_element_type=jnp.float32)
+            total = part if total is None else total + part
+            sums = jnp.sum(weights.astype(jnp.float32), axis=1, keepdims=True)
+            denominator = sums if denominator is None else denominator + sums
         for head in range(heads):
-            own = jnp.where(lane == head, q, jnp.bfloat16(0))
-            columns = slice(2 * head * VD, (2 * head + 2) * VD)
-            total = None
-            for block in range(index + 1):
-                rows = slice(2 * block * length, 2 * (block + 1) * length)
-                scores = lax.dot_general(
-                    own, k_all[rows, :], (((1,), (1,)), ((), ())), preferred_element_type=jnp.float32
-                )
-                raised = scores + 1.0
-                weights = raised * raised + 1.0
-                if block == index:
-                    weights = jnp.where(seen, weights, 0.0)
-                part = jnp.dot(
-                    weights.astype(jnp.bfloat16), v_all[rows, columns], preferred_element_type=jnp.float32
-                )
-                total = part if total is None else total + part
-            o_all[index * count : (index + 1) * count, head * VD : (head + 1) * VD] = (
-                total[:, :VD] / total[:, VD:]
-            ).astype(jnp.bfloat16)
+            own = slice(head * count, (head + 1) * count)
+            lanes = slice(head * VD, (head + 1) * VD)
+            o_all[index * count : (index + 1) * count, lanes] = (total[own, lanes] / denominator[own]).astype(
+                jnp.bfloat16
+            )
 
 
 def deal(o_all, outs, chip):
@@ -145,7 +150,6 @@
     length, count = k_all.shape[0] // (2 * chips), q_part.shape[0] // chips
     _, rows_of = stacks(count, mine[0].shape[1] // wide_k)
     chip, core = seat()
-    ones = jnp.ones((length, VD), jnp.bfloat16)
     for turn in range(chips):
         there = chip ^ turn
         for tile, (at, size) in enumerate(rows_of):
@@ -155,10 +159,7 @@
         for ref, side in ((mine[turn], core), (partner[turn], 1 - core)):
             rows = pl.ds(pl.multiple_of((2 * there + side) * length, length), length)
             k_all[rows, :] = ref[:length, :wide_k]
-            for head in range(heads):
-                at = wide_k + head * VD
-                v_all[rows, 2 * head * VD : (2 * head + 1) * VD] = ref[:length, at : at + VD]
-                v_all[rows, (2 * head + 1) * VD : (2 * head + 2) * VD] = ones
+            v_all[rows, :] = ref[:length, wide_k:]
     attend_rows(q_part, k_all, v_all, o_all, 0, core, chips, heads)
     deal(o_all, outs, chip)
 
@@ -185,7 +186,7 @@
         out_shape=(
             *(pltpu.VMEM((first, heads * VD), kind),) * chips,
             pltpu.VMEM((whole, heads * KD), kind),
-            pltpu.VMEM((whole, 2 * heads * VD), kind),
+            pltpu.VMEM((whole, heads * VD), kind),
         ),
         scratch_shapes=scratch(first),
         compiler_params=room(20),

time: 83.2 us -> 82.9 us (level)
  no operation moved by 1% of the time
where the time goes in v2:
time: 82.9 us; the launch traced here: 82.6 us
  starting transfers between devices  36.6 us (44%)
  waiting for transfers between devices  32.4 us (39%)
  Pallas kernels  13.2 us (16%)
    ppermute x11, starting transfers between devices, hop(): return lax.ppermute(value, 'head', pairs)  21 us
    ppermute x11, waiting for transfers between devices, hop(): return lax.ppermute(value, 'head', pairs)  18.7 us
    ppermute x16, starting transfers between devices, swap(): return lax.ppermute(value, axis, [(i, i ^ bits) for i in range(count)])  15.7 us
    ppermute x16, waiting for transfers between devices, swap(): return lax.ppermute(value, axis, [(i, i ^ bits) for i in range(count)])  13.7 us
    pallas_call x1, Pallas kernels, stage(): pl.pallas_call(stage_kernel, out_shape=pltpu.VMEM(weight.shape, weight.dt...  3.39 us
    pallas_call x4, Pallas kernels, project(): pl.pallas_call(functools.partial(project_kernel, chips=len(chunks[0]), ch...  3.2 us
    pallas_call x1, Pallas kernels, attend(): pl.pallas_call(functools.partial(attend_first_kernel, chips=chips, heads=...  1.95 us
    pallas_call x1, Pallas kernels, attend(): pl.pallas_call(functools.partial(attend_later_kernel, chips=chips, heads=...  1.88 us
  transfers between devices with their start and end apart: 27, of which 10 were waited for; matrix products, arithmetic and copies ran while one was open for 0% of the time, Pallas kernels for 11%

profile of v2, /device:TPU:0, one launch (start us, length us, event | category | flops | bytes accessed | tf_op | source)
XLA Modules:
  0.0 82.6 jit_solution(3680935466002186427)
XLA Ops:
  0.0 1.5 %pack.1 = (bf16[304,384]{1,0:T(8,128)(2,1)S(1)}, bf16[304,384]{1,0:T(8,128)(2,1)S(1)}, bf16[304,384]{1,0:T(8,128)(2,1)S(1)}, bf16[304,384]{1,0:T(8,128)(2,1)S(1)...) custom-call(bf16[256,512]{1,0:T(8,128)(2,1)} %q_ref.1, ...), custom_call_target="tpu_custom_call" | custom-call | tf_op jit(solution)/shard_map/pack/pallas_call | solution.py:74
  1.5 3.0 %collective-permute-start = (bf16[304,384]{1,0:T(8,128)(2,1)S(1)}, bf16[304,384]{1,0:T(8,128)(2,1)S(1)}, u32[]{:S(2)}, u32[]{:S(2)}) collective-permute-start(bf16[304,384]{1,0:T(8,128)(2,1)S(1)} %get-tuple-element.28), channel_id=1, source_target_pairs={{0,8},{4,12},{8,0},{12,4},{16,24},{20,28},{24,16},{28,20},{1,9},{5... | collective-permute-start | bytes 700424 | tf_op jit(solution)/shard_map/ppermute | solution.py:17
  4.6 1.5 %collective-permute-start.1 = (bf16[304,384]{1,0:T(8,128)(2,1)S(1)}, bf16[304,384]{1,0:T(8,128)(2,1)S(1)}, u32[]{:S(2)}, u32[]{:S(2)}) collective-permute-start(bf16[304,384]{1,0:T(8,128)(2,1)S(1)} %get-tuple-element.29), channel_id=1, source_target_pairs={{0,16},{4,20},{8,24},{12,28},{16,0},{20,4},{24,8},{28,12},{1,17},{... | collective-permute-start | bytes 700424 | tf_op jit(solution)/shard_map/ppermute | solution.py:17
  6.1 0.0 collective-permute-start.2
  6.1 0.0 collective-permute-start.3
  6.1 5.0 %collective-permute-done.refs_1_ = bf16[304,384]{1,0:T(8,128)(2,1)S(1)} collective-permute-done((bf16[304,384]{1,0:T(8,128)(2,1)S(1)}, bf16[304,384]{1,0:T(8,128)(2,1)S(1)}, u32[]{:S(2)}, u32[]{:S(2)}) %collective-permute-start) | collective-permute-done | bytes 233504 | tf_op jit(solution)/shard_map/ppermute | solution.py:17
  11.1 0.0 collective-permute-start.4
  11.1 5.6 %collective-permute-done.1.refs_2_ = bf16[304,384]{1,0:T(8,128)(2,1)S(1)} collective-permute-done((bf16[304,384]{1,0:T(8,128)(2,1)S(1)}, bf16[304,384]{1,0:T(8,128)(2,1)S(1)}, u32[]{:S(2)}, u32[]{:S(2)}) %collective-permute-start.1) | collective-permute-done | bytes 233504 | tf_op jit(solution)/shard_map/ppermute | solution.py:17
  16.7 0.0 collective-permute-start.5
  16.7 0.0 collective-permute-done.2.refs_3_
  16.7 0.5 collective-permute-start.6
  17.2 0.0 collective-permute-done.3.refs_4_
  17.2 0.0 collective-permute-done.4.refs_5_
  17.2 1.0 %collective-permute-done.5.refs_6_ = bf16[304,384]{1,0:T(8,128)(2,1)S(1)} collective-permute-done((bf16[304,384]{1,0:T(8,128)(2,1)S(1)}, bf16[304,384]{1,0:T(8,128)(2,1)S(1)}, u32[]{:S(2)}, u32[]{:S(2)}) %collective-permute-start.5) | collective-permute-done | bytes 233504 | tf_op jit(solution)/shard_map/ppermute | solution.py:17
  18.2 0.3 collective-permute-done.6.refs_7_
  18.6 1.9 %attend0.1 = (bf16[128,256]{1,0:T(8,128)(2,1)S(1)}, bf16[128,256]{1,0:T(8,128)(2,1)S(1)}, bf16[128,256]{1,0:T(8,128)(2,1)S(1)}, bf16[128,256]{1,0:T(8,128)(2,1)S...) custom-call(bf16[304,384]{1,0:T(8,128)(2,1)S(1)} %get-tuple-element.27.refs_0_, ...), custom_call_target="tpu_custom_call" | custom-call | tf_op jit(solution)/shard_map/attend0/pallas_call | solution.py:184
  20.5 1.0 %collective-permute-start.7 = (bf16[128,256]{1,0:T(8,128)(2,1)S(1)}, bf16[128,256]{1,0:T(8,128)(2,1)S(1)}, u32[]{:S(2)}, u32[]{:S(2)}) collective-permute-start(bf16[128,256]{1,0:T(8,128)(2,1)S(1)} %get-tuple-element.32), channel_id=1, source_target_pairs={{0,8},{4,12},{8,0},{12,4},{16,24},{20,28},{24,16},{28,20},{1,9},{5... | collective-permute-start | bytes 196616 | tf_op jit(solution)/shard_map/ppermute | solution.py:17
  21.5 1.1 %collective-permute-start.10 = (bf16[128,128]{1,0:T(8,128)(2,1)S(1)}, bf16[128,128]{1,0:T(8,128)(2,1)S(1)}, u32[]{:S(2)}, u32[]{:S(2)}) collective-permute-start(bf16[128,128]{1,0:T(8,128)(2,1)S(1)} %get-tuple-element.38), channel_id=1, source_target_pairs={{0,8},{4,12},{8,0},{12,4},{16,24},{20,28},{24,16},{28,20},{1,9},{5... | collective-permute-start | bytes 98312 | tf_op jit(solution)/shard_map/ppermute | solution.py:17
  22.6 1.5 %collective-permute-start.11 = (bf16[128,128]{1,0:T(8,128)(2,1)S(1)}, bf16[128,128]{1,0:T(8,128)(2,1)S(1)}, u32[]{:S(2)}, u32[]{:S(2)}) collective-permute-start(bf16[128,128]{1,0:T(8,128)(2,1)S(1)} %get-tuple-element.39), channel_id=1, source_target_pairs={{0,16},{4,20},{8,24},{12,28},{16,0},{20,4},{24,8},{28,12},{1,17},{... | collective-permute-start | bytes 98312 | tf_op jit(solution)/shard_map/ppermute | solution.py:17
  24.1 0.8 %collective-permute-start.12 = (bf16[128,128]{1,0:T(8,128)(2,1)S(1)}, bf16[128,128]{1,0:T(8,128)(2,1)S(1)}, u32[]{:S(2)}, u32[]{:S(2)}) collective-permute-start(bf16[128,128]{1,0:T(8,128)(2,1)S(1)} %get-tuple-element.40), channel_id=1, source_target_pairs={{0,24},{4,28},{8,16},{12,20},{16,8},{20,12},{24,0},{28,4},{1,25},{... | collective-permute-start | bytes 98312 | tf_op jit(solution)/shard_map/ppermute | solution.py:17
  25.0 1.2 %collective-permute-start.8 = (bf16[128,256]{1,0:T(8,128)(2,1)S(1)}, bf16[128,256]{1,0:T(8,128)(2,1)S(1)}, u32[]{:S(2)}, u32[]{:S(2)}) collective-permute-start(bf16[128,256]{1,0:T(8,128)(2,1)S(1)} %get-tuple-element.33), channel_id=1, source_target_pairs={{0,16},{4,20},{8,24},{12,28},{16,0},{20,4},{24,8},{28,12},{1,17},{... | collective-permute-start | bytes 196616 | tf_op jit(solution)/shard_map/ppermute | solution.py:17
  26.1 0.0 collective-permute-done.10.refs_1_
  26.1 1.4 %collective-permute-start.9 = (bf16[128,256]{1,0:T(8,128)(2,1)S(1)}, bf16[128,256]{1,0:T(8,128)(2,1)S(1)}, u32[]{:S(2)}, u32[]{:S(2)}) collective-permute-start(bf16[128,256]{1,0:T(8,128)(2,1)S(1)} %get-tuple-element.34), channel_id=1, source_target_pairs={{0,24},{4,28},{8,16},{12,20},{16,8},{20,12},{24,0},{28,4},{1,25},{... | collective-permute-start | bytes 196616 | tf_op jit(solution)/shard_map/ppermute | solution.py:17
  27.6 0.0 collective-permute-done.11.refs_2_
  27.6 1.8 %collective-permute-done.12.refs_3_ = bf16[128,128]{1,0:T(8,128)(2,1)S(1)} collective-permute-done((bf16[128,128]{1,0:T(8,128)(2,1)S(1)}, bf16[128,128]{1,0:T(8,128)(2,1)S(1)}, u32[]{:S(2)}, u32[]{:S(2)}) %collective-permute-start.12) | collective-permute-done | bytes 32800 | tf_op jit(solution)/shard_map/ppermute | solution.py:17
  29.4 1.9 %attend1.1 = (bf16[128,256]{1,0:T(8,128)(2,1)S(1)}, bf16[128,256]{1,0:T(8,128)(2,1)S(1)}, bf16[128,256]{1,0:T(8,128)(2,1)S(1)}, bf16[128,256]{1,0:T(8,128)(2,1)S(1)}) custom-call(bf16[2048,128]{1,0:T(8,128)(2,1)S(1)} %get-tuple-element.35.k_all, bf16[2048,256]{1,0:T(8,128)(2,1)S(1)} %get-tuple-element.36.v_all, ...), custom_call_target="tpu_custom_call" | custom-call | tf_op jit(solution)/shard_map/attend1/pallas_call | solution.py:195
  31.2 0.2 collective-permute-start.13
  31.4 0.9 %collective-permute-start.14 = (bf16[128,256]{1,0:T(8,128)(2,1)S(1)}, bf16[128,256]{1,0:T(8,128)(2,1)S(1)}, u32[]{:S(2)}, u32[]{:S(2)}) collective-permute-start(bf16[128,256]{1,0:T(8,128)(2,1)S(1)} %get-tuple-element.43), channel_id=1, source_target_pairs={{0,16},{4,20},{8,24},{12,28},{16,0},{20,4},{24,8},{28,12},{1,17},{... | collective-permute-start | bytes 196616 | tf_op jit(solution)/shard_map/ppermute | solution.py:17
  32.3 0.0 collective-permute-done.7.refs_1_
  32.3 2.5 %collective-permute-start.15 = (bf16[128,256]{1,0:T(8,128)(2,1)S(1)}, bf16[128,256]{1,0:T(8,128)(2,1)S(1)}, u32[]{:S(2)}, u32[]{:S(2)}) collective-permute-start(bf16[128,256]{1,0:T(8,128)(2,1)S(1)} %get-tuple-element.44), channel_id=1, source_target_pairs={{0,24},{4,28},{8,16},{12,20},{16,8},{20,12},{24,0},{28,4},{1,25},{... | collective-permute-start | bytes 196616 | tf_op jit(solution)/shard_map/ppermute | solution.py:17
  34.8 3.4 %stage.1.refs_8_.refs_4_ = bf16[1024,4096]{1,0:T(8,128)(2,1)S(1)} custom-call(bf16[1024,4096]{1,0:T(8,128)(2,1)} %w_ref.1), custom_call_target="tpu_custom_call" | custom-call | tf_op jit(solution)/shard_map/stage/pallas_call | solution.py:94
  38.2 0.0 collective-permute-done.8.refs_2_
  38.2 0.0 collective-permute-done.9.refs_3_
  38.2 0.5 shard_map.48.one
  38.7 3.5 %collective-permute-start.19 = (bf16[128,1024]{1,0:T(8,128)(2,1)S(1)}, bf16[128,1024]{1,0:T(8,128)(2,1)S(1)}, u32[]{:S(2)}, u32[]{:S(2)}) collective-permute-start(bf16[128,1024]{1,0:T(8,128)(2,1)S(1)} %shard_map.48.one), channel_id=1, source_target_pairs={{0,1},{3,2},{4,5},{7,6},{8,9},{11,10},{12,13},{15,14},{16,17},{19,... | collective-permute-start | bytes 786440 | tf_op jit(solution)/shard_map/ppermute | solution.py:309
  42.2 0.0 collective-permute-done.14.refs_6_.refs_2_
  42.2 0.0 collective-permute-done.15.refs_7_.refs_3_
  42.2 1.8 %shard_map.46 = (bf16[128,1024]{1,0:T(8,128)(2,1)S(1)}, bf16[128,1024]{1,0:T(8,128)(2,1)S(1)}, bf16[256,1024]{1,0:T(8,128)(2,1)S(1)}, f32[256,1024]{1,0:T(8,128)S(1)}) custom-call(bf16[128,256]{1,0:T(8,128)(2,1)S(1)} %get-tuple-element.31.refs_0_, bf16[128,256]{1,0:T(8,128)(2,1)S(1)} %collective-permute-done.7.refs_1_, ...), custom_call_target="tpu_custom_call" | custom-call | tf_op jit(solution)/shard_map/pallas_call | solution.py:235
  44.0 1.3 %collective-permute-start.22 = (bf16[128,1024]{1,0:T(8,128)(2,1)S(1)}, bf16[128,1024]{1,0:T(8,128)(2,1)S(1)}, u32[]{:S(2)}, u32[]{:S(2)}) collective-permute-start(bf16[128,1024]{1,0:T(8,128)(2,1)S(1)} %get-tuple-element.47.one), channel_id=1, source_target_pairs={{0,1},{3,2},{4,5},{7,6},{8,9},{11,10},{12,13},{15,14},{16,17},{19,... | collective-permute-start | bytes 786440 | tf_op jit(solution)/shard_map/ppermute | solution.py:309
  45.4 0.5 shard_map.47.one
  45.8 1.3 %collective-permute-start.17 = (bf16[128,1024]{1,0:T(8,128)(2,1)S(1)}, bf16[128,1024]{1,0:T(8,128)(2,1)S(1)}, u32[]{:S(2)}, u32[]{:S(2)}) collective-permute-start(bf16[128,1024]{1,0:T(8,128)(2,1)S(1)} %shard_map.47.one), channel_id=1, source_target_pairs={{0,1},{3,2},{4,5},{7,6},{8,9},{11,10},{12,13},{15,14},{16,17},{19,... | collective-permute-start | bytes 786440 | tf_op jit(solution)/shard_map/ppermute | solution.py:309
  47.1 1.3 %collective-permute-start.24 = (bf16[128,1024]{1,0:T(8,128)(2,1)S(1)}, bf16[128,1024]{1,0:T(8,128)(2,1)S(1)}, u32[]{:S(2)}, u32[]{:S(2)}) collective-permute-start(bf16[128,1024]{1,0:T(8,128)(2,1)S(1)} %get-tuple-element.48), channel_id=1, source_target_pairs={{2,3},{1,0},{6,7},{5,4},{10,11},{9,8},{14,15},{13,12},{18,19},{17,... | collective-permute-start | bytes 786440 | tf_op jit(solution)/shard_map/ppermute | solution.py:309
  48.4 0.5 shard_map.49.one
  48.9 4.6 %collective-permute-start.25 = (bf16[128,1024]{1,0:T(8,128)(2,1)S(1)}, bf16[128,1024]{1,0:T(8,128)(2,1)S(1)}, u32[]{:S(2)}, u32[]{:S(2)}) collective-permute-start(bf16[128,1024]{1,0:T(8,128)(2,1)S(1)} %shard_map.49.one), channel_id=1, source_target_pairs={{0,1},{3,2},{4,5},{7,6},{8,9},{11,10},{12,13},{15,14},{16,17},{19,... | collective-permute-start | bytes 786440 | tf_op jit(solution)/shard_map/ppermute | solution.py:309
  53.5 0.1 join.6
  53.6 0.7 collective-permute-start.20
  54.3 0.2 collective-permute-done.22.other
  54.5 4.4 %collective-permute-start.16 = (bf16[256,1024]{1,0:T(8,128)(2,1)S(1)}, bf16[256,1024]{1,0:T(8,128)(2,1)S(1)}, u32[]{:S(2)}, u32[]{:S(2)}) collective-permute-start(bf16[256,1024]{1,0:T(8,128)(2,1)S(1)} %get-tuple-element.46.one), channel_id=1, source_target_pairs={{0,1},{3,2},{4,5},{7,6},{8,9},{11,10},{12,13},{15,14},{16,17},{19,... | collective-permute-start | bytes 1572872 | tf_op jit(solution)/shard_map/ppermute | solution.py:309
  58.9 0.1 join.8
  59.0 1.1 %collective-permute-done.17.other = bf16[128,1024]{1,0:T(8,128)(2,1)S(1)} collective-permute-done((bf16[128,1024]{1,0:T(8,128)(2,1)S(1)}, bf16[128,1024]{1,0:T(8,128)(2,1)S(1)}, u32[]{:S(2)}, u32[]{:S(2)}) %collective-permute-start.17) | collective-permute-done | bytes 262176 | tf_op jit(solution)/shard_map/ppermute | solution.py:309
  60.1 0.7 collective-permute-start.23
  60.8 0.1 join.5
  60.8 4.9 %collective-permute-done.25.other = bf16[128,1024]{1,0:T(8,128)(2,1)S(1)} collective-permute-done((bf16[128,1024]{1,0:T(8,128)(2,1)S(1)}, bf16[128,1024]{1,0:T(8,128)(2,1)S(1)}, u32[]{:S(2)}, u32[]{:S(2)}) %collective-permute-start.25) | collective-permute-done | bytes 262176 | tf_op jit(solution)/shard_map/ppermute | solution.py:309
  65.7 0.7 collective-permute-start.18
  66.4 0.1 join.9
  66.5 0.0 collective-permute-done.20.other
  66.5 1.3 %collective-permute-start.26 = (bf16[128,1024]{1,0:T(8,128)(2,1)S(1)}, bf16[128,1024]{1,0:T(8,128)(2,1)S(1)}, u32[]{:S(2)}, u32[]{:S(2)}) collective-permute-start(bf16[128,1024]{1,0:T(8,128)(2,1)S(1)} %join.9), channel_id=1, source_target_pairs={{1,3},{2,0},{5,7},{6,4},{9,11},{10,8},{13,15},{14,12},{17,19},{18,... | collective-permute-start | bytes 786440 | tf_op jit(solution)/shard_map/ppermute | solution.py:309
  67.8 0.1 join.7
  67.8 0.0 collective-permute-done.24.refs_3_
  67.8 1.3 %collective-permute-start.21 = (bf16[128,1024]{1,0:T(8,128)(2,1)S(1)}, bf16[128,1024]{1,0:T(8,128)(2,1)S(1)}, u32[]{:S(2)}, u32[]{:S(2)}) collective-permute-start(bf16[128,1024]{1,0:T(8,128)(2,1)S(1)} %join.7), channel_id=1, source_target_pairs={{2,3},{1,0},{6,7},{5,4},{10,11},{9,8},{14,15},{13,12},{18,19},{17,... | collective-permute-start | bytes 786440 | tf_op jit(solution)/shard_map/ppermute | solution.py:309
  69.2 10.0 %collective-permute-done.26.refs_4_ = bf16[128,1024]{1,0:T(8,128)(2,1)S(1)} collective-permute-done((bf16[128,1024]{1,0:T(8,128)(2,1)S(1)}, bf16[128,1024]{1,0:T(8,128)(2,1)S(1)}, u32[]{:S(2)}, u32[]{:S(2)}) %collective-permute-start.26) | collective-permute-done | bytes 262176 | tf_op jit(solution)/shard_map/ppermute | solution.py:309
  79.2 0.0 collective-permute-done.16.third
  79.2 2.4 %collective-permute-done.21.refs_1_ = bf16[128,1024]{1,0:T(8,128)(2,1)S(1)} collective-permute-done((bf16[128,1024]{1,0:T(8,128)(2,1)S(1)}, bf16[128,1024]{1,0:T(8,128)(2,1)S(1)}, u32[]{:S(2)}, u32[]{:S(2)}) %collective-permute-start.21) | collective-permute-done | bytes 262176 | tf_op jit(solution)/shard_map/ppermute | solution.py:309
  81.6 1.0 %finish.1 = bf16[256,1024]{1,0:T(8,128)(2,1)} custom-call(f32[256,1024]{1,0:T(8,128)S(1)} %get-tuple-element.45.own, bf16[256,1024]{1,0:T(8,128)(2,1)S(1)} %collective-permute-done.16.third, bf16[128,1024]{1,0:T(8,128)(2,1)S(1)} %collective-permute-done.18.refs_0_, bf16[128,1024]{1,0:T(8,128)(2,1)S(1)} %collective-permute-done.21.refs_1_, ...), custom_call_target="tpu_custom_call" | custom-call | tf_op jit(solution)/shard_map/finish/pallas_call | solution.py:278
  (4 shorter events, 0.0 us)
Async XLA Ops:
  1.5 9.6 %collective-permute-start = (bf16[304,384]{1,0:T(8,128)(2,1)S(1)}, bf16[304,384]{1,0:T(8,128)(2,1)S(1)}, u32[]{:S(2)}, u32[]{:S(2)}) collective-permute-start(bf16[304,384]{1,0:T(8,128)(2,1)S(1)} %get-tuple-element.28), channel_id=1, source_target_pairs={{0,8},{4,12},{8,0},{12,4},{16,24},{20,28},{24,16},{28,20},{1,9},{5... | collective-permute-start | bytes 700424 | tf_op jit(solution)/shard_map/ppermute | solution.py:17
  4.6 12.2 %collective-permute-start.1 = (bf16[304,384]{1,0:T(8,128)(2,1)S(1)}, bf16[304,384]{1,0:T(8,128)(2,1)S(1)}, u32[]{:S(2)}, u32[]{:S(2)}) collective-permute-start(bf16[304,384]{1,0:T(8,128)(2,1)S(1)} %get-tuple-element.29), channel_id=1, source_target_pairs={{0,16},{4,20},{8,24},{12,28},{16,0},{20,4},{24,8},{28,12},{1,17},{... | collective-permute-start | bytes 700424 | tf_op jit(solution)/shard_map/ppermute | solution.py:17
  6.1 10.6 %collective-permute-start.2 = (bf16[304,384]{1,0:T(8,128)(2,1)S(1)}, bf16[304,384]{1,0:T(8,128)(2,1)S(1)}, u32[]{:S(2)}, u32[]{:S(2)}) collective-permute-start(bf16[304,384]{1,0:T(8,128)(2,1)S(1)} %get-tuple-element.30), channel_id=1, source_target_pairs={{0,24},{4,28},{8,16},{12,20},{16,8},{20,12},{24,0},{28,4},{1,25},{... | collective-permute-start | bytes 700424 | tf_op jit(solution)/shard_map/ppermute | solution.py:17
  6.1 11.1 %collective-permute-start.3 = (bf16[304,384]{1,0:T(8,128)(2,1)S(1)}, bf16[304,384]{1,0:T(8,128)(2,1)S(1)}, u32[]{:S(2)}, u32[]{:S(2)}) collective-permute-start(bf16[304,384]{1,0:T(8,128)(2,1)S(1)} %get-tuple-element.27.refs_0_), channel_id=1, source_target_pairs={{0,4},{4,0},{8,12},{12,8},{16,20},{20,16},{24,28},{28,24},{1,5},{5... | collective-permute-start | bytes 700424 | tf_op jit(solution)/shard_map/ppermute | solution.py:17
  11.1 6.1 %collective-permute-start.4 = (bf16[304,384]{1,0:T(8,128)(2,1)S(1)}, bf16[304,384]{1,0:T(8,128)(2,1)S(1)}, u32[]{:S(2)}, u32[]{:S(2)}) collective-permute-start(bf16[304,384]{1,0:T(8,128)(2,1)S(1)} %collective-permute-done.refs_1_), channel_id=1, source_target_pairs={{0,4},{4,0},{8,12},{12,8},{16,20},{20,16},{24,28},{28,24},{1,5},{5... | collective-permute-start | bytes 700424 | tf_op jit(solution)/shard_map/ppermute | solution.py:17
  16.7 1.5 %collective-permute-start.5 = (bf16[304,384]{1,0:T(8,128)(2,1)S(1)}, bf16[304,384]{1,0:T(8,128)(2,1)S(1)}, u32[]{:S(2)}, u32[]{:S(2)}) collective-permute-start(bf16[304,384]{1,0:T(8,128)(2,1)S(1)} %collective-permute-done.1.refs_2_), channel_id=1, source_target_pairs={{0,4},{4,0},{8,12},{12,8},{16,20},{20,16},{24,28},{28,24},{1,5},{5... | collective-permute-start | bytes 700424 | tf_op jit(solution)/shard_map/ppermute | solution.py:17
  16.7 1.8 %collective-permute-start.6 = (bf16[304,384]{1,0:T(8,128)(2,1)S(1)}, bf16[304,384]{1,0:T(8,128)(2,1)S(1)}, u32[]{:S(2)}, u32[]{:S(2)}) collective-permute-start(bf16[304,384]{1,0:T(8,128)(2,1)S(1)} %collective-permute-done.2.refs_3_), channel_id=1, source_target_pairs={{0,4},{4,0},{8,12},{12,8},{16,20},{20,16},{24,28},{28,24},{1,5},{5... | collective-permute-start | bytes 700424 | tf_op jit(solution)/shard_map/ppermute | solution.py:17
  20.5 11.8 %collective-permute-start.7 = (bf16[128,256]{1,0:T(8,128)(2,1)S(1)}, bf16[128,256]{1,0:T(8,128)(2,1)S(1)}, u32[]{:S(2)}, u32[]{:S(2)}) collective-permute-start(bf16[128,256]{1,0:T(8,128)(2,1)S(1)} %get-tuple-element.32), channel_id=1, source_target_pairs={{0,8},{4,12},{8,0},{12,4},{16,24},{20,28},{24,16},{28,20},{1,9},{5... | collective-permute-start | bytes 196616 | tf_op jit(solution)/shard_map/ppermute | solution.py:17
  21.5 4.7 %collective-permute-start.10 = (bf16[128,128]{1,0:T(8,128)(2,1)S(1)}, bf16[128,128]{1,0:T(8,128)(2,1)S(1)}, u32[]{:S(2)}, u32[]{:S(2)}) collective-permute-start(bf16[128,128]{1,0:T(8,128)(2,1)S(1)} %get-tuple-element.38), channel_id=1, source_target_pairs={{0,8},{4,12},{8,0},{12,4},{16,24},{20,28},{24,16},{28,20},{1,9},{5... | collective-permute-start | bytes 98312 | tf_op jit(solution)/shard_map/ppermute | solution.py:17
  22.6 5.0 %collective-permute-start.11 = (bf16[128,128]{1,0:T(8,128)(2,1)S(1)}, bf16[128,128]{1,0:T(8,128)(2,1)S(1)}, u32[]{:S(2)}, u32[]{:S(2)}) collective-permute-start(bf16[128,128]{1,0:T(8,128)(2,1)S(1)} %get-tuple-element.39), channel_id=1, source_target_pairs={{0,16},{4,20},{8,24},{12,28},{16,0},{20,4},{24,8},{28,12},{1,17},{... | collective-permute-start | bytes 98312 | tf_op jit(solution)/shard_map/ppermute | solution.py:17
  24.1 5.2 %collective-permute-start.12 = (bf16[128,128]{1,0:T(8,128)(2,1)S(1)}, bf16[128,128]{1,0:T(8,128)(2,1)S(1)}, u32[]{:S(2)}, u32[]{:S(2)}) collective-permute-start(bf16[128,128]{1,0:T(8,128)(2,1)S(1)} %get-tuple-element.40), channel_id=1, source_target_pairs={{0,24},{4,28},{8,16},{12,20},{16,8},{20,12},{24,0},{28,4},{1,25},{... | collective-permute-start | bytes 98312 | tf_op jit(solution)/shard_map/ppermute | solution.py:17
  25.0 13.2 %collective-permute-start.8 = (bf16[128,256]{1,0:T(8,128)(2,1)S(1)}, bf16[128,256]{1,0:T(8,128)(2,1)S(1)}, u32[]{:S(2)}, u32[]{:S(2)}) collective-permute-start(bf16[128,256]{1,0:T(8,128)(2,1)S(1)} %get-tuple-element.33), channel_id=1, source_target_pairs={{0,16},{4,20},{8,24},{12,28},{16,0},{20,4},{24,8},{28,12},{1,17},{... | collective-permute-start | bytes 196616 | tf_op jit(solution)/shard_map/ppermute | solution.py:17
  26.1 12.1 %collective-permute-start.9 = (bf16[128,256]{1,0:T(8,128)(2,1)S(1)}, bf16[128,256]{1,0:T(8,128)(2,1)S(1)}, u32[]{:S(2)}, u32[]{:S(2)}) collective-permute-start(bf16[128,256]{1,0:T(8,128)(2,1)S(1)} %get-tuple-element.34), channel_id=1, source_target_pairs={{0,24},{4,28},{8,16},{12,20},{16,8},{20,12},{24,0},{28,4},{1,25},{... | collective-permute-start | bytes 196616 | tf_op jit(solution)/shard_map/ppermute | solution.py:17
  31.2 10.9 %collective-permute-start.13 = (bf16[128,256]{1,0:T(8,128)(2,1)S(1)}, bf16[128,256]{1,0:T(8,128)(2,1)S(1)}, u32[]{:S(2)}, u32[]{:S(2)}) collective-permute-start(bf16[128,256]{1,0:T(8,128)(2,1)S(1)} %get-tuple-element.42), channel_id=1, source_target_pairs={{0,8},{4,12},{8,0},{12,4},{16,24},{20,28},{24,16},{28,20},{1,9},{5... | collective-permute-start | bytes 196616 | tf_op jit(solution)/shard_map/ppermute | solution.py:17
  31.4 10.8 %collective-permute-start.14 = (bf16[128,256]{1,0:T(8,128)(2,1)S(1)}, bf16[128,256]{1,0:T(8,128)(2,1)S(1)}, u32[]{:S(2)}, u32[]{:S(2)}) collective-permute-start(bf16[128,256]{1,0:T(8,128)(2,1)S(1)} %get-tuple-element.43), channel_id=1, source_target_pairs={{0,16},{4,20},{8,24},{12,28},{16,0},{20,4},{24,8},{28,12},{1,17},{... | collective-permute-start | bytes 196616 | tf_op jit(solution)/shard_map/ppermute | solution.py:17
  32.3 9.9 %collective-permute-start.15 = (bf16[128,256]{1,0:T(8,128)(2,1)S(1)}, bf16[128,256]{1,0:T(8,128)(2,1)S(1)}, u32[]{:S(2)}, u32[]{:S(2)}) collective-permute-start(bf16[128,256]{1,0:T(8,128)(2,1)S(1)} %get-tuple-element.44), channel_id=1, source_target_pairs={{0,24},{4,28},{8,16},{12,20},{16,8},{20,12},{24,0},{28,4},{1,25},{... | collective-permute-start | bytes 196616 | tf_op jit(solution)/shard_map/ppermute | solution.py:17
  38.7 14.8 %collective-permute-start.19 = (bf16[128,1024]{1,0:T(8,128)(2,1)S(1)}, bf16[128,1024]{1,0:T(8,128)(2,1)S(1)}, u32[]{:S(2)}, u32[]{:S(2)}) collective-permute-start(bf16[128,1024]{1,0:T(8,128)(2,1)S(1)} %shard_map.48.one), channel_id=1, source_target_pairs={{0,1},{3,2},{4,5},{7,6},{8,9},{11,10},{12,13},{15,14},{16,17},{19,... | collective-permute-start | bytes 786440 | tf_op jit(solution)/shard_map/ppermute | solution.py:309
  44.0 10.4 %collective-permute-start.22 = (bf16[128,1024]{1,0:T(8,128)(2,1)S(1)}, bf16[128,1024]{1,0:T(8,128)(2,1)S(1)}, u32[]{:S(2)}, u32[]{:S(2)}) collective-permute-start(bf16[128,1024]{1,0:T(8,128)(2,1)S(1)} %get-tuple-element.47.one), channel_id=1, source_target_pairs={{0,1},{3,2},{4,5},{7,6},{8,9},{11,10},{12,13},{15,14},{16,17},{19,... | collective-permute-start | bytes 786440 | tf_op jit(solution)/shard_map/ppermute | solution.py:309
  45.8 14.3 %collective-permute-start.17 = (bf16[128,1024]{1,0:T(8,128)(2,1)S(1)}, bf16[128,1024]{1,0:T(8,128)(2,1)S(1)}, u32[]{:S(2)}, u32[]{:S(2)}) collective-permute-start(bf16[128,1024]{1,0:T(8,128)(2,1)S(1)} %shard_map.47.one), channel_id=1, source_target_pairs={{0,1},{3,2},{4,5},{7,6},{8,9},{11,10},{12,13},{15,14},{16,17},{19,... | collective-permute-start | bytes 786440 | tf_op jit(solution)/shard_map/ppermute | solution.py:309
  47.1 20.7 %collective-permute-start.24 = (bf16[128,1024]{1,0:T(8,128)(2,1)S(1)}, bf16[128,1024]{1,0:T(8,128)(2,1)S(1)}, u32[]{:S(2)}, u32[]{:S(2)}) collective-permute-start(bf16[128,1024]{1,0:T(8,128)(2,1)S(1)} %get-tuple-element.48), channel_id=1, source_target_pairs={{2,3},{1,0},{6,7},{5,4},{10,11},{9,8},{14,15},{13,12},{18,19},{17,... | collective-permute-start | bytes 786440 | tf_op jit(solution)/shard_map/ppermute | solution.py:309
  48.9 16.8 %collective-permute-start.25 = (bf16[128,1024]{1,0:T(8,128)(2,1)S(1)}, bf16[128,1024]{1,0:T(8,128)(2,1)S(1)}, u32[]{:S(2)}, u32[]{:S(2)}) collective-permute-start(bf16[128,1024]{1,0:T(8,128)(2,1)S(1)} %shard_map.49.one), channel_id=1, source_target_pairs={{0,1},{3,2},{4,5},{7,6},{8,9},{11,10},{12,13},{15,14},{16,17},{19,... | collective-permute-start | bytes 786440 | tf_op jit(solution)/shard_map/ppermute | solution.py:309
  53.6 12.9 %collective-permute-start.20 = (bf16[128,1024]{1,0:T(8,128)(2,1)S(1)}, bf16[128,1024]{1,0:T(8,128)(2,1)S(1)}, u32[]{:S(2)}, u32[]{:S(2)}) collective-permute-start(bf16[128,1024]{1,0:T(8,128)(2,1)S(1)} %join.6), channel_id=1, source_target_pairs={{1,2},{2,1},{5,6},{6,5},{9,10},{10,9},{13,14},{14,13},{17,18},{18,... | collective-permute-start | bytes 786440 | tf_op jit(solution)/shard_map/ppermute | solution.py:309
  54.5 24.7 %collective-permute-start.16 = (bf16[256,1024]{1,0:T(8,128)(2,1)S(1)}, bf16[256,1024]{1,0:T(8,128)(2,1)S(1)}, u32[]{:S(2)}, u32[]{:S(2)}) collective-permute-start(bf16[256,1024]{1,0:T(8,128)(2,1)S(1)} %get-tuple-element.46.one), channel_id=1, source_target_pairs={{0,1},{3,2},{4,5},{7,6},{8,9},{11,10},{12,13},{15,14},{16,17},{19,... | collective-permute-start | bytes 1572872 | tf_op jit(solution)/shard_map/ppermute | solution.py:309
  60.1 9.1 %collective-permute-start.23 = (bf16[128,1024]{1,0:T(8,128)(2,1)S(1)}, bf16[128,1024]{1,0:T(8,128)(2,1)S(1)}, u32[]{:S(2)}, u32[]{:S(2)}) collective-permute-start(bf16[128,1024]{1,0:T(8,128)(2,1)S(1)} %join.8), channel_id=1, source_target_pairs={{1,2},{2,1},{5,6},{6,5},{9,10},{10,9},{13,14},{14,13},{17,18},{18,... | collective-permute-start | bytes 786440 | tf_op jit(solution)/shard_map/ppermute | solution.py:309
  65.7 3.4 %collective-permute-start.18 = (bf16[128,1024]{1,0:T(8,128)(2,1)S(1)}, bf16[128,1024]{1,0:T(8,128)(2,1)S(1)}, u32[]{:S(2)}, u32[]{:S(2)}) collective-permute-start(bf16[128,1024]{1,0:T(8,128)(2,1)S(1)} %join.5), channel_id=1, source_target_pairs={{1,2},{2,1},{5,6},{6,5},{9,10},{10,9},{13,14},{14,13},{17,18},{18,... | collective-permute-start | bytes 786440 | tf_op jit(solution)/shard_map/ppermute | solution.py:309
  66.5 12.7 %collective-permute-start.26 = (bf16[128,1024]{1,0:T(8,128)(2,1)S(1)}, bf16[128,1024]{1,0:T(8,128)(2,1)S(1)}, u32[]{:S(2)}, u32[]{:S(2)}) collective-permute-start(bf16[128,1024]{1,0:T(8,128)(2,1)S(1)} %join.9), channel_id=1, source_target_pairs={{1,3},{2,0},{5,7},{6,4},{9,11},{10,8},{13,15},{14,12},{17,19},{18,... | collective-permute-start | bytes 786440 | tf_op jit(solution)/shard_map/ppermute | solution.py:309
  67.8 13.7 %collective-permute-start.21 = (bf16[128,1024]{1,0:T(8,128)(2,1)S(1)}, bf16[128,1024]{1,0:T(8,128)(2,1)S(1)}, u32[]{:S(2)}, u32[]{:S(2)}) collective-permute-start(bf16[128,1024]{1,0:T(8,128)(2,1)S(1)} %join.7), channel_id=1, source_target_pairs={{2,3},{1,0},{6,7},{5,4},{10,11},{9,8},{14,15},{13,12},{18,19},{17,... | collective-permute-start | bytes 786440 | tf_op jit(solution)/shard_map/ppermute | solution.py:309

commit v3 on v2

--- a/solution.py
+++ b/solution.py
@@ -204,7 +204,7 @@
 
 def block_at(slot):
     rank = lax.axis_index("head")
-    turns = [(3, 3, 0, 0), (2, 2, 1, 1), (1, 0, 3, 2), (0, 1, 2, 3)][slot]
+    turns = [(3, 3, 0, 0), (2, 2, 1, 1), (1, 0, 3, 2), (0, 1, 2, 3), (2, 0, 3, 1)][slot]
     block = jnp.int32(turns[0])
     for other in range(1, 4):
         block = jnp.where(rank == other, jnp.int32(turns[other]), block)
@@ -258,11 +258,16 @@
 
 def finish_kernel(own, third, *refs, cuts, arrivals):
     out, rows, sent = refs[-3:]
+    rank = lax.axis_index("head")
+    edge = (rank == 0) | (rank == 3)
     copies, at = [], 0
     for low, high, count in zip(cuts, cuts[1:], arrivals):
         total = own[low:high, :] + third[low:high, :].astype(jnp.float32)
-        for part in refs[at : at + count]:
+        for part in refs[at : at + min(count, 2)]:
             total = total + part[...].astype(jnp.float32)
+        if count == 3:
+            beside = refs[at + 2][...].astype(jnp.float32)
+            total = total + jnp.where(edge, beside, jnp.zeros_like(beside))
         at += count
         rows[low:high, :] = total.astype(rows.dtype)
         copies.append(
@@ -312,17 +317,18 @@
     (to_first[0],) = project(chunks[:1], weight, columns, ((0, (0,)),), (bf16,))
     (to_second[0],) = project(chunks[:1], weight, columns, ((1, (0,)),), (bf16,))
     (to_first[1],) = project(chunks[1:], weight, columns, ((0, (0,)),), (bf16,))
-    beside, to_second[1], to_third, own = project(
-        chunks, weight, columns, ((2, (1,)), (1, (1,)), (2, (0, 1)), (3, (0, 1))), (bf16, bf16, bf16, f32)
+    both_ways, to_second[1], to_third, own = project(
+        chunks, weight, columns, ((4, (1,)), (1, (1,)), (2, (0, 1)), (3, (0, 1))), (bf16, bf16, bf16, f32)
     )
     first = [hop(value, 0, 1) for value in to_first]
-    second = [hop(value, 0, 1) for value in to_second]
+    second = [hop(to_second[0], 0, 1)]
+    second.append(lax.ppermute(both_ways, "head", [(0, 1), (1, 0), (2, 3), (3, 2)]))
     third = hop(to_third, 0, 1)
     joined = [join(mine, other, 0) for mine, other in zip(to_first, first)]
     late = [hop(join(mine, other, 0), 1, 2) for mine, other in zip(to_second, second)]
     last = hop(join(to_third, hop(joined[0], 1, 2), 0), 2, 3)
-    straight, beside = hop(joined[1], 1, 3), hop(beside, 2, 3)
-    return finish(own, third, ((late[0], last), (late[1], beside, straight)), cuts)
+    straight = hop(joined[1], 1, 3)
+    return finish(own, third, ((late[0], last), (late[1], straight, second[1])), cuts)
 
 
 def gathered(queries, key_vectors, value_vectors, out_weight):

time: 82.9 us -> 82.5 us (level)
  starting transfers between devices: 36.6 us -> 33.3 us
  waiting for transfers between devices: 32.4 us -> 35.5 us
    ppermute x16, waiting for transfers between devices: 13.7 us -> 19.3 us  [swap(): return lax.ppermute(value, axis, [(i, i ^ bits) for i in range(count)])]
    ppermute x11 -> x9, starting transfers between devices: 21 us -> 17.4 us  [hop(): return lax.ppermute(value, 'head', pairs)]
    ppermute x11 -> x9, waiting for transfers between devices: 18.7 us -> 16.2 us  [hop(): return lax.ppermute(value, 'head', pairs)]
  transfers between devices with their start and end apart: 27 -> 26, of which waited for: 10 -> 15; matrix products, arithmetic and copies ran while one was open for 0% -> 0% of each run, Pallas kernels for 11% -> 10%
where the time goes in v3:
time: 82.5 us; the launch traced here: 82.2 us
  waiting for transfers between devices  35.5 us (43%)
  starting transfers between devices  33.3 us (40%)
  Pallas kernels  13.2 us (16%)
    ppermute x16, waiting for transfers between devices, swap(): return lax.ppermute(value, axis, [(i, i ^ bits) for i in range(count)])  19.3 us
    ppermute x9, starting transfers between devices, hop(): return lax.ppermute(value, 'head', pairs)  17.4 us
    ppermute x9, waiting for transfers between devices, hop(): return lax.ppermute(value, 'head', pairs)  16.2 us
    ppermute x16, starting transfers between devices, swap(): return lax.ppermute(value, axis, [(i, i ^ bits) for i in range(count)])  15.7 us
    pallas_call x1, Pallas kernels, stage(): pl.pallas_call(stage_kernel, out_shape=pltpu.VMEM(weight.shape, weight.dt...  3.39 us
    pallas_call x4, Pallas kernels, project(): pl.pallas_call(functools.partial(project_kernel, chips=len(chunks[0]), ch...  3.16 us
    pallas_call x1, Pallas kernels, attend(): pl.pallas_call(functools.partial(attend_first_kernel, chips=chips, heads=...  1.95 us
    pallas_call x1, Pallas kernels, attend(): pl.pallas_call(functools.partial(attend_later_kernel, chips=chips, heads=...  1.88 us
  transfers between devices with their start and end apart: 26, of which 15 were waited for; matrix products, arithmetic and copies ran while one was open for 0% of the time, Pallas kernels for 10%

profile of v3, /device:TPU:0, one launch (start us, length us, event | category | flops | bytes accessed | tf_op | source)
XLA Modules:
  0.0 82.2 jit_solution(1361802939636415726)
XLA Ops:
  0.0 1.5 %pack.1 = (bf16[304,384]{1,0:T(8,128)(2,1)S(1)}, bf16[304,384]{1,0:T(8,128)(2,1)S(1)}, bf16[304,384]{1,0:T(8,128)(2,1)S(1)}, bf16[304,384]{1,0:T(8,128)(2,1)S(1)...) custom-call(bf16[256,512]{1,0:T(8,128)(2,1)} %q_ref.1, ...), custom_call_target="tpu_custom_call" | custom-call | tf_op jit(solution)/shard_map/pack/pallas_call | solution.py:74
  1.5 3.0 %collective-permute-start = (bf16[304,384]{1,0:T(8,128)(2,1)S(1)}, bf16[304,384]{1,0:T(8,128)(2,1)S(1)}, u32[]{:S(2)}, u32[]{:S(2)}) collective-permute-start(bf16[304,384]{1,0:T(8,128)(2,1)S(1)} %get-tuple-element.28), channel_id=1, source_target_pairs={{0,8},{4,12},{8,0},{12,4},{16,24},{20,28},{24,16},{28,20},{1,9},{5... | collective-permute-start | bytes 700424 | tf_op jit(solution)/shard_map/ppermute | solution.py:17
  4.6 1.5 %collective-permute-start.1 = (bf16[304,384]{1,0:T(8,128)(2,1)S(1)}, bf16[304,384]{1,0:T(8,128)(2,1)S(1)}, u32[]{:S(2)}, u32[]{:S(2)}) collective-permute-start(bf16[304,384]{1,0:T(8,128)(2,1)S(1)} %get-tuple-element.29), channel_id=1, source_target_pairs={{0,16},{4,20},{8,24},{12,28},{16,0},{20,4},{24,8},{28,12},{1,17},{... | collective-permute-start | bytes 700424 | tf_op jit(solution)/shard_map/ppermute | solution.py:17
  6.1 0.0 collective-permute-start.2
  6.1 0.0 collective-permute-start.3
  6.1 5.0 %collective-permute-done.refs_1_ = bf16[304,384]{1,0:T(8,128)(2,1)S(1)} collective-permute-done((bf16[304,384]{1,0:T(8,128)(2,1)S(1)}, bf16[304,384]{1,0:T(8,128)(2,1)S(1)}, u32[]{:S(2)}, u32[]{:S(2)}) %collective-permute-start) | collective-permute-done | bytes 233504 | tf_op jit(solution)/shard_map/ppermute | solution.py:17
  11.1 0.0 collective-permute-start.4
  11.1 5.6 %collective-permute-done.1.refs_2_ = bf16[304,384]{1,0:T(8,128)(2,1)S(1)} collective-permute-done((bf16[304,384]{1,0:T(8,128)(2,1)S(1)}, bf16[304,384]{1,0:T(8,128)(2,1)S(1)}, u32[]{:S(2)}, u32[]{:S(2)}) %collective-permute-start.1) | collective-permute-done | bytes 233504 | tf_op jit(solution)/shard_map/ppermute | solution.py:17
  16.7 0.0 collective-permute-start.5
  16.7 0.0 collective-permute-done.2.refs_3_
  16.7 0.5 collective-permute-start.6
  17.2 0.0 collective-permute-done.3.refs_4_
  17.2 0.0 collective-permute-done.4.refs_5_
  17.2 1.0 %collective-permute-done.5.refs_6_ = bf16[304,384]{1,0:T(8,128)(2,1)S(1)} collective-permute-done((bf16[304,384]{1,0:T(8,128)(2,1)S(1)}, bf16[304,384]{1,0:T(8,128)(2,1)S(1)}, u32[]{:S(2)}, u32[]{:S(2)}) %collective-permute-start.5) | collective-permute-done | bytes 233504 | tf_op jit(solution)/shard_map/ppermute | solution.py:17
  18.2 0.3 collective-permute-done.6.refs_7_
  18.6 1.9 %attend0.1 = (bf16[128,256]{1,0:T(8,128)(2,1)S(1)}, bf16[128,256]{1,0:T(8,128)(2,1)S(1)}, bf16[128,256]{1,0:T(8,128)(2,1)S(1)}, bf16[128,256]{1,0:T(8,128)(2,1)S...) custom-call(bf16[304,384]{1,0:T(8,128)(2,1)S(1)} %get-tuple-element.27.refs_0_, ...), custom_call_target="tpu_custom_call" | custom-call | tf_op jit(solution)/shard_map/attend0/pallas_call | solution.py:184
  20.5 1.0 %collective-permute-start.7 = (bf16[128,256]{1,0:T(8,128)(2,1)S(1)}, bf16[128,256]{1,0:T(8,128)(2,1)S(1)}, u32[]{:S(2)}, u32[]{:S(2)}) collective-permute-start(bf16[128,256]{1,0:T(8,128)(2,1)S(1)} %get-tuple-element.32), channel_id=1, source_target_pairs={{0,8},{4,12},{8,0},{12,4},{16,24},{20,28},{24,16},{28,20},{1,9},{5... | collective-permute-start | bytes 196616 | tf_op jit(solution)/shard_map/ppermute | solution.py:17
  21.5 1.2 %collective-permute-start.8 = (bf16[128,256]{1,0:T(8,128)(2,1)S(1)}, bf16[128,256]{1,0:T(8,128)(2,1)S(1)}, u32[]{:S(2)}, u32[]{:S(2)}) collective-permute-start(bf16[128,256]{1,0:T(8,128)(2,1)S(1)} %get-tuple-element.33), channel_id=1, source_target_pairs={{0,16},{4,20},{8,24},{12,28},{16,0},{20,4},{24,8},{28,12},{1,17},{... | collective-permute-start | bytes 196616 | tf_op jit(solution)/shard_map/ppermute | solution.py:17
  22.6 1.4 %collective-permute-start.9 = (bf16[128,256]{1,0:T(8,128)(2,1)S(1)}, bf16[128,256]{1,0:T(8,128)(2,1)S(1)}, u32[]{:S(2)}, u32[]{:S(2)}) collective-permute-start(bf16[128,256]{1,0:T(8,128)(2,1)S(1)} %get-tuple-element.34), channel_id=1, source_target_pairs={{0,24},{4,28},{8,16},{12,20},{16,8},{20,12},{24,0},{28,4},{1,25},{... | collective-permute-start | bytes 196616 | tf_op jit(solution)/shard_map/ppermute | solution.py:17
  24.1 3.4 %stage.1.refs_8_.refs_4_ = bf16[1024,4096]{1,0:T(8,128)(2,1)S(1)} custom-call(bf16[1024,4096]{1,0:T(8,128)(2,1)} %w_ref.1), custom_call_target="tpu_custom_call" | custom-call | tf_op jit(solution)/shard_map/stage/pallas_call | solution.py:94
  27.5 0.0 collective-permute-done.7.refs_1_
  27.5 0.3 collective-permute-done.9.refs_3_
  27.8 0.4 shard_map.48.one
  28.3 3.5 %collective-permute-start.19 = (bf16[128,1024]{1,0:T(8,128)(2,1)S(1)}, bf16[128,1024]{1,0:T(8,128)(2,1)S(1)}, u32[]{:S(2)}, u32[]{:S(2)}) collective-permute-start(bf16[128,1024]{1,0:T(8,128)(2,1)S(1)} %shard_map.48.one), channel_id=1, source_target_pairs={{0,1},{3,2},{4,5},{7,6},{8,9},{11,10},{12,13},{15,14},{16,17},{19,... | collective-permute-start | bytes 786440 | tf_op jit(solution)/shard_map/ppermute | solution.py:314
  31.8 1.5 %collective-permute-start.10 = (bf16[128,128]{1,0:T(8,128)(2,1)S(1)}, bf16[128,128]{1,0:T(8,128)(2,1)S(1)}, u32[]{:S(2)}, u32[]{:S(2)}) collective-permute-start(bf16[128,128]{1,0:T(8,128)(2,1)S(1)} %get-tuple-element.38), channel_id=1, source_target_pairs={{0,8},{4,12},{8,0},{12,4},{16,24},{20,28},{24,16},{28,20},{1,9},{5... | collective-permute-start | bytes 98312 | tf_op jit(solution)/shard_map/ppermute | solution.py:17
  33.3 0.5 collective-permute-start.11
  33.8 1.5 %collective-permute-start.12 = (bf16[128,128]{1,0:T(8,128)(2,1)S(1)}, bf16[128,128]{1,0:T(8,128)(2,1)S(1)}, u32[]{:S(2)}, u32[]{:S(2)}) collective-permute-start(bf16[128,128]{1,0:T(8,128)(2,1)S(1)} %get-tuple-element.40), channel_id=1, source_target_pairs={{0,24},{4,28},{8,16},{12,20},{16,8},{20,12},{24,0},{28,4},{1,25},{... | collective-permute-start | bytes 98312 | tf_op jit(solution)/shard_map/ppermute | solution.py:17
  35.3 0.4 collective-permute-done.10.refs_1_
  35.7 1.5 %collective-permute-done.11.refs_2_ = bf16[128,128]{1,0:T(8,128)(2,1)S(1)} collective-permute-done((bf16[128,128]{1,0:T(8,128)(2,1)S(1)}, bf16[128,128]{1,0:T(8,128)(2,1)S(1)}, u32[]{:S(2)}, u32[]{:S(2)}) %collective-permute-start.11) | collective-permute-done | bytes 32800 | tf_op jit(solution)/shard_map/ppermute | solution.py:17
  37.2 1.4 %collective-permute-done.12.refs_3_ = bf16[128,128]{1,0:T(8,128)(2,1)S(1)} collective-permute-done((bf16[128,128]{1,0:T(8,128)(2,1)S(1)}, bf16[128,128]{1,0:T(8,128)(2,1)S(1)}, u32[]{:S(2)}, u32[]{:S(2)}) %collective-permute-start.12) | collective-permute-done | bytes 32800 | tf_op jit(solution)/shard_map/ppermute | solution.py:17
  38.6 1.9 %attend1.1 = (bf16[128,256]{1,0:T(8,128)(2,1)S(1)}, bf16[128,256]{1,0:T(8,128)(2,1)S(1)}, bf16[128,256]{1,0:T(8,128)(2,1)S(1)}, bf16[128,256]{1,0:T(8,128)(2,1)S(1)}) custom-call(bf16[2048,128]{1,0:T(8,128)(2,1)S(1)} %get-tuple-element.35.k_all, bf16[2048,256]{1,0:T(8,128)(2,1)S(1)} %get-tuple-element.36.v_all, ...), custom_call_target="tpu_custom_call" | custom-call | tf_op jit(solution)/shard_map/attend1/pallas_call | solution.py:195
  40.5 1.3 %collective-permute-start.13 = (bf16[128,256]{1,0:T(8,128)(2,1)S(1)}, bf16[128,256]{1,0:T(8,128)(2,1)S(1)}, u32[]{:S(2)}, u32[]{:S(2)}) collective-permute-start(bf16[128,256]{1,0:T(8,128)(2,1)S(1)} %get-tuple-element.42), channel_id=1, source_target_pairs={{0,8},{4,12},{8,0},{12,4},{16,24},{20,28},{24,16},{28,20},{1,9},{5... | collective-permute-start | bytes 196616 | tf_op jit(solution)/shard_map/ppermute | solution.py:17
  41.8 0.8 %collective-permute-start.14 = (bf16[128,256]{1,0:T(8,128)(2,1)S(1)}, bf16[128,256]{1,0:T(8,128)(2,1)S(1)}, u32[]{:S(2)}, u32[]{:S(2)}) collective-permute-start(bf16[128,256]{1,0:T(8,128)(2,1)S(1)} %get-tuple-element.43), channel_id=1, source_target_pairs={{0,16},{4,20},{8,24},{12,28},{16,0},{20,4},{24,8},{28,12},{1,17},{... | collective-permute-start | bytes 196616 | tf_op jit(solution)/shard_map/ppermute | solution.py:17
  42.7 1.4 %collective-permute-start.15 = (bf16[128,256]{1,0:T(8,128)(2,1)S(1)}, bf16[128,256]{1,0:T(8,128)(2,1)S(1)}, u32[]{:S(2)}, u32[]{:S(2)}) collective-permute-start(bf16[128,256]{1,0:T(8,128)(2,1)S(1)} %get-tuple-element.44), channel_id=1, source_target_pairs={{0,24},{4,28},{8,16},{12,20},{16,8},{20,12},{24,0},{28,4},{1,25},{... | collective-permute-start | bytes 196616 | tf_op jit(solution)/shard_map/ppermute | solution.py:17
  44.1 0.8 collective-permute-done.13.refs_5_.refs_1_
  44.8 1.3 %collective-permute-done.14.refs_6_.refs_2_ = bf16[128,256]{1,0:T(8,128)(2,1)S(1)} collective-permute-done((bf16[128,256]{1,0:T(8,128)(2,1)S(1)}, bf16[128,256]{1,0:T(8,128)(2,1)S(1)}, u32[]{:S(2)}, u32[]{:S(2)}) %collective-permute-start.14) | collective-permute-done | bytes 65568 | tf_op jit(solution)/shard_map/ppermute | solution.py:17
  46.1 1.7 %collective-permute-done.15.refs_7_.refs_3_ = bf16[128,256]{1,0:T(8,128)(2,1)S(1)} collective-permute-done((bf16[128,256]{1,0:T(8,128)(2,1)S(1)}, bf16[128,256]{1,0:T(8,128)(2,1)S(1)}, u32[]{:S(2)}, u32[]{:S(2)}) %collective-permute-start.15) | collective-permute-done | bytes 65568 | tf_op jit(solution)/shard_map/ppermute | solution.py:17
  47.8 1.8 %shard_map.46 = (bf16[128,1024]{1,0:T(8,128)(2,1)S(1)}, bf16[128,1024]{1,0:T(8,128)(2,1)S(1)}, bf16[256,1024]{1,0:T(8,128)(2,1)S(1)}, f32[256,1024]{1,0:T(8,128)S(1)}) custom-call(bf16[128,256]{1,0:T(8,128)(2,1)S(1)} %get-tuple-element.31.refs_0_, bf16[128,256]{1,0:T(8,128)(2,1)S(1)} %collective-permute-done.7.refs_1_, ...), custom_call_target="tpu_custom_call" | custom-call | tf_op jit(solution)/shard_map/pallas_call | solution.py:235
  49.6 0.1 collective-permute-start.22
  49.7 0.5 shard_map.47.one
  50.2 3.9 %collective-permute-start.17 = (bf16[128,1024]{1,0:T(8,128)(2,1)S(1)}, bf16[128,1024]{1,0:T(8,128)(2,1)S(1)}, u32[]{:S(2)}, u32[]{:S(2)}) collective-permute-start(bf16[128,1024]{1,0:T(8,128)(2,1)S(1)} %shard_map.47.one), channel_id=1, source_target_pairs={{0,1},{3,2},{4,5},{7,6},{8,9},{11,10},{12,13},{15,14},{16,17},{19,... | collective-permute-start | bytes 786440 | tf_op jit(solution)/shard_map/ppermute | solution.py:314
  54.1 0.5 shard_map.49.one
  54.6 1.3 %collective-permute-start.24 = (bf16[128,1024]{1,0:T(8,128)(2,1)S(1)}, bf16[128,1024]{1,0:T(8,128)(2,1)S(1)}, u32[]{:S(2)}, u32[]{:S(2)}) collective-permute-start(bf16[128,1024]{1,0:T(8,128)(2,1)S(1)} %shard_map.49.one), channel_id=1, source_target_pairs={{0,1},{3,2},{4,5},{7,6},{8,9},{11,10},{12,13},{15,14},{16,17},{19,... | collective-permute-start | bytes 786440 | tf_op jit(solution)/shard_map/ppermute | solution.py:314
  55.9 0.0 collective-permute-done.19.other
  55.9 0.1 join.6
  56.0 0.7 collective-permute-start.20
  56.7 4.1 %collective-permute-start.16 = (bf16[256,1024]{1,0:T(8,128)(2,1)S(1)}, bf16[256,1024]{1,0:T(8,128)(2,1)S(1)}, u32[]{:S(2)}, u32[]{:S(2)}) collective-permute-start(bf16[256,1024]{1,0:T(8,128)(2,1)S(1)} %get-tuple-element.46.one), channel_id=1, source_target_pairs={{0,1},{3,2},{4,5},{7,6},{8,9},{11,10},{12,13},{15,14},{16,17},{19,... | collective-permute-start | bytes 1572872 | tf_op jit(solution)/shard_map/ppermute | solution.py:314
  60.8 0.1 join.8
  60.8 0.7 collective-permute-start.23
  61.5 0.5 collective-permute-done.17.other
  62.0 0.1 join.5
  62.1 0.7 collective-permute-start.18
  62.8 4.9 %collective-permute-done.24.other = bf16[128,1024]{1,0:T(8,128)(2,1)S(1)} collective-permute-done((bf16[128,1024]{1,0:T(8,128)(2,1)S(1)}, bf16[128,1024]{1,0:T(8,128)(2,1)S(1)}, u32[]{:S(2)}, u32[]{:S(2)}) %collective-permute-start.24) | collective-permute-done | bytes 262176 | tf_op jit(solution)/shard_map/ppermute | solution.py:314
  67.6 0.1 join.9
  67.7 1.3 %collective-permute-start.25 = (bf16[128,1024]{1,0:T(8,128)(2,1)S(1)}, bf16[128,1024]{1,0:T(8,128)(2,1)S(1)}, u32[]{:S(2)}, u32[]{:S(2)}) collective-permute-start(bf16[128,1024]{1,0:T(8,128)(2,1)S(1)} %join.9), channel_id=1, source_target_pairs={{1,3},{2,0},{5,7},{6,4},{9,11},{10,8},{13,15},{14,12},{17,19},{18,... | collective-permute-start | bytes 786440 | tf_op jit(solution)/shard_map/ppermute | solution.py:314
  69.0 0.0 collective-permute-done.20.other
  69.0 0.1 join.7
  69.1 1.3 %collective-permute-start.21 = (bf16[128,1024]{1,0:T(8,128)(2,1)S(1)}, bf16[128,1024]{1,0:T(8,128)(2,1)S(1)}, u32[]{:S(2)}, u32[]{:S(2)}) collective-permute-start(bf16[128,1024]{1,0:T(8,128)(2,1)S(1)} %join.7), channel_id=1, source_target_pairs={{2,3},{1,0},{6,7},{5,4},{10,11},{9,8},{14,15},{13,12},{18,19},{17,... | collective-permute-start | bytes 786440 | tf_op jit(solution)/shard_map/ppermute | solution.py:314
  70.4 0.0 collective-permute-done.23.refs_2_
  70.4 0.0 collective-permute-done.18.refs_0_
  70.4 8.3 %collective-permute-done.25.refs_3_ = bf16[128,1024]{1,0:T(8,128)(2,1)S(1)} collective-permute-done((bf16[128,1024]{1,0:T(8,128)(2,1)S(1)}, bf16[128,1024]{1,0:T(8,128)(2,1)S(1)}, u32[]{:S(2)}, u32[]{:S(2)}) %collective-permute-start.25) | collective-permute-done | bytes 262176 | tf_op jit(solution)/shard_map/ppermute | solution.py:314
  78.7 0.0 collective-permute-done.16.third
  78.7 2.5 %collective-permute-done.21.refs_1_ = bf16[128,1024]{1,0:T(8,128)(2,1)S(1)} collective-permute-done((bf16[128,1024]{1,0:T(8,128)(2,1)S(1)}, bf16[128,1024]{1,0:T(8,128)(2,1)S(1)}, u32[]{:S(2)}, u32[]{:S(2)}) %collective-permute-start.21) | collective-permute-done | bytes 262176 | tf_op jit(solution)/shard_map/ppermute | solution.py:314
  81.2 1.0 %finish.1 = bf16[256,1024]{1,0:T(8,128)(2,1)} custom-call(f32[256,1024]{1,0:T(8,128)S(1)} %get-tuple-element.45.own, bf16[256,1024]{1,0:T(8,128)(2,1)S(1)} %collective-permute-done.16.third, bf16[128,1024]{1,0:T(8,128)(2,1)S(1)} %collective-permute-done.18.refs_0_, bf16[128,1024]{1,0:T(8,128)(2,1)S(1)} %collective-permute-done.21.refs_1_, ...), custom_call_target="tpu_custom_call" | custom-call | tf_op jit(solution)/shard_map/finish/pallas_call | solution.py:283
  (2 shorter events, 0.0 us)
Async XLA Ops:
  1.5 9.6 %collective-permute-start = (bf16[304,384]{1,0:T(8,128)(2,1)S(1)}, bf16[304,384]{1,0:T(8,128)(2,1)S(1)}, u32[]{:S(2)}, u32[]{:S(2)}) collective-permute-start(bf16[304,384]{1,0:T(8,128)(2,1)S(1)} %get-tuple-element.28), channel_id=1, source_target_pairs={{0,8},{4,12},{8,0},{12,4},{16,24},{20,28},{24,16},{28,20},{1,9},{5... | collective-permute-start | bytes 700424 | tf_op jit(solution)/shard_map/ppermute | solution.py:17
  4.6 12.2 %collective-permute-start.1 = (bf16[304,384]{1,0:T(8,128)(2,1)S(1)}, bf16[304,384]{1,0:T(8,128)(2,1)S(1)}, u32[]{:S(2)}, u32[]{:S(2)}) collective-permute-start(bf16[304,384]{1,0:T(8,128)(2,1)S(1)} %get-tuple-element.29), channel_id=1, source_target_pairs={{0,16},{4,20},{8,24},{12,28},{16,0},{20,4},{24,8},{28,12},{1,17},{... | collective-permute-start | bytes 700424 | tf_op jit(solution)/shard_map/ppermute | solution.py:17
  6.1 10.6 %collective-permute-start.2 = (bf16[304,384]{1,0:T(8,128)(2,1)S(1)}, bf16[304,384]{1,0:T(8,128)(2,1)S(1)}, u32[]{:S(2)}, u32[]{:S(2)}) collective-permute-start(bf16[304,384]{1,0:T(8,128)(2,1)S(1)} %get-tuple-element.30), channel_id=1, source_target_pairs={{0,24},{4,28},{8,16},{12,20},{16,8},{20,12},{24,0},{28,4},{1,25},{... | collective-permute-start | bytes 700424 | tf_op jit(solution)/shard_map/ppermute | solution.py:17
  6.1 11.1 %collective-permute-start.3 = (bf16[304,384]{1,0:T(8,128)(2,1)S(1)}, bf16[304,384]{1,0:T(8,128)(2,1)S(1)}, u32[]{:S(2)}, u32[]{:S(2)}) collective-permute-start(bf16[304,384]{1,0:T(8,128)(2,1)S(1)} %get-tuple-element.27.refs_0_), channel_id=1, source_target_pairs={{0,4},{4,0},{8,12},{12,8},{16,20},{20,16},{24,28},{28,24},{1,5},{5... | collective-permute-start | bytes 700424 | tf_op jit(solution)/shard_map/ppermute | solution.py:17
  11.1 6.1 %collective-permute-start.4 = (bf16[304,384]{1,0:T(8,128)(2,1)S(1)}, bf16[304,384]{1,0:T(8,128)(2,1)S(1)}, u32[]{:S(2)}, u32[]{:S(2)}) collective-permute-start(bf16[304,384]{1,0:T(8,128)(2,1)S(1)} %collective-permute-done.refs_1_), channel_id=1, source_target_pairs={{0,4},{4,0},{8,12},{12,8},{16,20},{20,16},{24,28},{28,24},{1,5},{5... | collective-permute-start | bytes 700424 | tf_op jit(solution)/shard_map/ppermute | solution.py:17
  16.7 1.5 %collective-permute-start.5 = (bf16[304,384]{1,0:T(8,128)(2,1)S(1)}, bf16[304,384]{1,0:T(8,128)(2,1)S(1)}, u32[]{:S(2)}, u32[]{:S(2)}) collective-permute-start(bf16[304,384]{1,0:T(8,128)(2,1)S(1)} %collective-permute-done.1.refs_2_), channel_id=1, source_target_pairs={{0,4},{4,0},{8,12},{12,8},{16,20},{20,16},{24,28},{28,24},{1,5},{5... | collective-permute-start | bytes 700424 | tf_op jit(solution)/shard_map/ppermute | solution.py:17
  16.7 1.8 %collective-permute-start.6 = (bf16[304,384]{1,0:T(8,128)(2,1)S(1)}, bf16[304,384]{1,0:T(8,128)(2,1)S(1)}, u32[]{:S(2)}, u32[]{:S(2)}) collective-permute-start(bf16[304,384]{1,0:T(8,128)(2,1)S(1)} %collective-permute-done.2.refs_3_), channel_id=1, source_target_pairs={{0,4},{4,0},{8,12},{12,8},{16,20},{20,16},{24,28},{28,24},{1,5},{5... | collective-permute-start | bytes 700424 | tf_op jit(solution)/shard_map/ppermute | solution.py:17
  20.5 7.0 %collective-permute-start.7 = (bf16[128,256]{1,0:T(8,128)(2,1)S(1)}, bf16[128,256]{1,0:T(8,128)(2,1)S(1)}, u32[]{:S(2)}, u32[]{:S(2)}) collective-permute-start(bf16[128,256]{1,0:T(8,128)(2,1)S(1)} %get-tuple-element.32), channel_id=1, source_target_pairs={{0,8},{4,12},{8,0},{12,4},{16,24},{20,28},{24,16},{28,20},{1,9},{5... | collective-permute-start | bytes 196616 | tf_op jit(solution)/shard_map/ppermute | solution.py:17
  21.5 6.0 %collective-permute-start.8 = (bf16[128,256]{1,0:T(8,128)(2,1)S(1)}, bf16[128,256]{1,0:T(8,128)(2,1)S(1)}, u32[]{:S(2)}, u32[]{:S(2)}) collective-permute-start(bf16[128,256]{1,0:T(8,128)(2,1)S(1)} %get-tuple-element.33), channel_id=1, source_target_pairs={{0,16},{4,20},{8,24},{12,28},{16,0},{20,4},{24,8},{28,12},{1,17},{... | collective-permute-start | bytes 196616 | tf_op jit(solution)/shard_map/ppermute | solution.py:17
  22.6 5.2 %collective-permute-start.9 = (bf16[128,256]{1,0:T(8,128)(2,1)S(1)}, bf16[128,256]{1,0:T(8,128)(2,1)S(1)}, u32[]{:S(2)}, u32[]{:S(2)}) collective-permute-start(bf16[128,256]{1,0:T(8,128)(2,1)S(1)} %get-tuple-element.34), channel_id=1, source_target_pairs={{0,24},{4,28},{8,16},{12,20},{16,8},{20,12},{24,0},{28,4},{1,25},{... | collective-permute-start | bytes 196616 | tf_op jit(solution)/shard_map/ppermute | solution.py:17
  28.3 27.6 %collective-permute-start.19 = (bf16[128,1024]{1,0:T(8,128)(2,1)S(1)}, bf16[128,1024]{1,0:T(8,128)(2,1)S(1)}, u32[]{:S(2)}, u32[]{:S(2)}) collective-permute-start(bf16[128,1024]{1,0:T(8,128)(2,1)S(1)} %shard_map.48.one), channel_id=1, source_target_pairs={{0,1},{3,2},{4,5},{7,6},{8,9},{11,10},{12,13},{15,14},{16,17},{19,... | collective-permute-start | bytes 786440 | tf_op jit(solution)/shard_map/ppermute | solution.py:314
  31.8 4.0 %collective-permute-start.10 = (bf16[128,128]{1,0:T(8,128)(2,1)S(1)}, bf16[128,128]{1,0:T(8,128)(2,1)S(1)}, u32[]{:S(2)}, u32[]{:S(2)}) collective-permute-start(bf16[128,128]{1,0:T(8,128)(2,1)S(1)} %get-tuple-element.38), channel_id=1, source_target_pairs={{0,8},{4,12},{8,0},{12,4},{16,24},{20,28},{24,16},{28,20},{1,9},{5... | collective-permute-start | bytes 98312 | tf_op jit(solution)/shard_map/ppermute | solution.py:17
  33.3 3.9 %collective-permute-start.11 = (bf16[128,128]{1,0:T(8,128)(2,1)S(1)}, bf16[128,128]{1,0:T(8,128)(2,1)S(1)}, u32[]{:S(2)}, u32[]{:S(2)}) collective-permute-start(bf16[128,128]{1,0:T(8,128)(2,1)S(1)} %get-tuple-element.39), channel_id=1, source_target_pairs={{0,16},{4,20},{8,24},{12,28},{16,0},{20,4},{24,8},{28,12},{1,17},{... | collective-permute-start | bytes 98312 | tf_op jit(solution)/shard_map/ppermute | solution.py:17
  33.8 4.8 %collective-permute-start.12 = (bf16[128,128]{1,0:T(8,128)(2,1)S(1)}, bf16[128,128]{1,0:T(8,128)(2,1)S(1)}, u32[]{:S(2)}, u32[]{:S(2)}) collective-permute-start(bf16[128,128]{1,0:T(8,128)(2,1)S(1)} %get-tuple-element.40), channel_id=1, source_target_pairs={{0,24},{4,28},{8,16},{12,20},{16,8},{20,12},{24,0},{28,4},{1,25},{... | collective-permute-start | bytes 98312 | tf_op jit(solution)/shard_map/ppermute | solution.py:17
  40.5 4.3 %collective-permute-start.13 = (bf16[128,256]{1,0:T(8,128)(2,1)S(1)}, bf16[128,256]{1,0:T(8,128)(2,1)S(1)}, u32[]{:S(2)}, u32[]{:S(2)}) collective-permute-start(bf16[128,256]{1,0:T(8,128)(2,1)S(1)} %get-tuple-element.42), channel_id=1, source_target_pairs={{0,8},{4,12},{8,0},{12,4},{16,24},{20,28},{24,16},{28,20},{1,9},{5... | collective-permute-start | bytes 196616 | tf_op jit(solution)/shard_map/ppermute | solution.py:17
  41.8 4.3 %collective-permute-start.14 = (bf16[128,256]{1,0:T(8,128)(2,1)S(1)}, bf16[128,256]{1,0:T(8,128)(2,1)S(1)}, u32[]{:S(2)}, u32[]{:S(2)}) collective-permute-start(bf16[128,256]{1,0:T(8,128)(2,1)S(1)} %get-tuple-element.43), channel_id=1, source_target_pairs={{0,16},{4,20},{8,24},{12,28},{16,0},{20,4},{24,8},{28,12},{1,17},{... | collective-permute-start | bytes 196616 | tf_op jit(solution)/shard_map/ppermute | solution.py:17
  42.7 5.2 %collective-permute-start.15 = (bf16[128,256]{1,0:T(8,128)(2,1)S(1)}, bf16[128,256]{1,0:T(8,128)(2,1)S(1)}, u32[]{:S(2)}, u32[]{:S(2)}) collective-permute-start(bf16[128,256]{1,0:T(8,128)(2,1)S(1)} %get-tuple-element.44), channel_id=1, source_target_pairs={{0,24},{4,28},{8,16},{12,20},{16,8},{20,12},{24,0},{28,4},{1,25},{... | collective-permute-start | bytes 196616 | tf_op jit(solution)/shard_map/ppermute | solution.py:17
  49.6 11.1 %collective-permute-start.22 = (bf16[128,1024]{1,0:T(8,128)(2,1)S(1)}, bf16[128,1024]{1,0:T(8,128)(2,1)S(1)}, u32[]{:S(2)}, u32[]{:S(2)}) collective-permute-start(bf16[128,1024]{1,0:T(8,128)(2,1)S(1)} %get-tuple-element.48), channel_id=1, source_target_pairs={{0,1},{1,0},{2,3},{3,2},{4,5},{5,4},{6,7},{7,6},{8,9},{9,8},{10,11... | collective-permute-start | bytes 786440 | tf_op jit(solution)/shard_map/ppermute | solution.py:325
  50.2 11.8 %collective-permute-start.17 = (bf16[128,1024]{1,0:T(8,128)(2,1)S(1)}, bf16[128,1024]{1,0:T(8,128)(2,1)S(1)}, u32[]{:S(2)}, u32[]{:S(2)}) collective-permute-start(bf16[128,1024]{1,0:T(8,128)(2,1)S(1)} %shard_map.47.one), channel_id=1, source_target_pairs={{0,1},{3,2},{4,5},{7,6},{8,9},{11,10},{12,13},{15,14},{16,17},{19,... | collective-permute-start | bytes 786440 | tf_op jit(solution)/shard_map/ppermute | solution.py:314
  54.6 13.1 %collective-permute-start.24 = (bf16[128,1024]{1,0:T(8,128)(2,1)S(1)}, bf16[128,1024]{1,0:T(8,128)(2,1)S(1)}, u32[]{:S(2)}, u32[]{:S(2)}) collective-permute-start(bf16[128,1024]{1,0:T(8,128)(2,1)S(1)} %shard_map.49.one), channel_id=1, source_target_pairs={{0,1},{3,2},{4,5},{7,6},{8,9},{11,10},{12,13},{15,14},{16,17},{19,... | collective-permute-start | bytes 786440 | tf_op jit(solution)/shard_map/ppermute | solution.py:314
  56.0 13.0 %collective-permute-start.20 = (bf16[128,1024]{1,0:T(8,128)(2,1)S(1)}, bf16[128,1024]{1,0:T(8,128)(2,1)S(1)}, u32[]{:S(2)}, u32[]{:S(2)}) collective-permute-start(bf16[128,1024]{1,0:T(8,128)(2,1)S(1)} %join.6), channel_id=1, source_target_pairs={{1,2},{2,1},{5,6},{6,5},{9,10},{10,9},{13,14},{14,13},{17,18},{18,... | collective-permute-start | bytes 786440 | tf_op jit(solution)/shard_map/ppermute | solution.py:314
  56.7 22.0 %collective-permute-start.16 = (bf16[256,1024]{1,0:T(8,128)(2,1)S(1)}, bf16[256,1024]{1,0:T(8,128)(2,1)S(1)}, u32[]{:S(2)}, u32[]{:S(2)}) collective-permute-start(bf16[256,1024]{1,0:T(8,128)(2,1)S(1)} %get-tuple-element.46.one), channel_id=1, source_target_pairs={{0,1},{3,2},{4,5},{7,6},{8,9},{11,10},{12,13},{15,14},{16,17},{19,... | collective-permute-start | bytes 1572872 | tf_op jit(solution)/shard_map/ppermute | solution.py:314
  60.8 9.5 %collective-permute-start.23 = (bf16[128,1024]{1,0:T(8,128)(2,1)S(1)}, bf16[128,1024]{1,0:T(8,128)(2,1)S(1)}, u32[]{:S(2)}, u32[]{:S(2)}) collective-permute-start(bf16[128,1024]{1,0:T(8,128)(2,1)S(1)} %join.8), channel_id=1, source_target_pairs={{1,2},{2,1},{5,6},{6,5},{9,10},{10,9},{13,14},{14,13},{17,18},{18,... | collective-permute-start | bytes 786440 | tf_op jit(solution)/shard_map/ppermute | solution.py:314
  62.1 8.3 %collective-permute-start.18 = (bf16[128,1024]{1,0:T(8,128)(2,1)S(1)}, bf16[128,1024]{1,0:T(8,128)(2,1)S(1)}, u32[]{:S(2)}, u32[]{:S(2)}) collective-permute-start(bf16[128,1024]{1,0:T(8,128)(2,1)S(1)} %join.5), channel_id=1, source_target_pairs={{1,2},{2,1},{5,6},{6,5},{9,10},{10,9},{13,14},{14,13},{17,18},{18,... | collective-permute-start | bytes 786440 | tf_op jit(solution)/shard_map/ppermute | solution.py:314
  67.7 11.0 %collective-permute-start.25 = (bf16[128,1024]{1,0:T(8,128)(2,1)S(1)}, bf16[128,1024]{1,0:T(8,128)(2,1)S(1)}, u32[]{:S(2)}, u32[]{:S(2)}) collective-permute-start(bf16[128,1024]{1,0:T(8,128)(2,1)S(1)} %join.9), channel_id=1, source_target_pairs={{1,3},{2,0},{5,7},{6,4},{9,11},{10,8},{13,15},{14,12},{17,19},{18,... | collective-permute-start | bytes 786440 | tf_op jit(solution)/shard_map/ppermute | solution.py:314
  69.1 12.1 %collective-permute-start.21 = (bf16[128,1024]{1,0:T(8,128)(2,1)S(1)}, bf16[128,1024]{1,0:T(8,128)(2,1)S(1)}, u32[]{:S(2)}, u32[]{:S(2)}) collective-permute-start(bf16[128,1024]{1,0:T(8,128)(2,1)S(1)} %join.7), channel_id=1, source_target_pairs={{2,3},{1,0},{6,7},{5,4},{10,11},{9,8},{14,15},{13,12},{18,19},{17,... | collective-permute-start | bytes 786440 | tf_op jit(solution)/shard_map/ppermute | solution.py:314
